TPU v7x, 512 devices: a whole 4x8x8 slice. The times are simulated.
512 devices in a mesh: seq: 32 (over z_hi, y, core), mp: 16 (over z_lo, x).
Axes of the slice: x: 4, y: 8, z: 8 (z_hi: 2, z_lo: 4; z = z_hi * 4 + z_lo), core: 2. Of those that a mesh axis runs over, the one named last changes fastest.
Arguments:
- inputs: bfloat16 [32768, 4096], P('seq', 'mp'), may hold values from -6 to 6
- conv_weight: bfloat16 [4, 4096], P(None, 'mp'), may hold values from -3 to 3
- conv_bias: bfloat16 [4096], P('mp'), may hold values from -3 to 3
- doc_start: int32 [32768], P('seq'), may hold values from 0 to 32767, as said below
- counts: int32 [32], P('seq'), may hold values from 341 to 1024
Outputs:
- gram: float32 [4096, 4096], P('seq', 'mp')
Inputs may be any that keep to these rules, and one draw needn't show every extreme that they name: doc_start is never above the token's own position, and for t > 0 either doc_start[t] == t or doc_start[t] == doc_start[t - 1]; doc_start[0] is 0.
All inputs are finite; a program needn't handle non-finite values.
Results may differ from a plain program's by a relative error of at most 0.0003.
Values may be sent and summed in bfloat16 or wider, within the bound.
No kernel may reach another device: no remote copies, remote signals or barrier semaphores. Data moves between devices by JAX's collectives and lax.ppermute only.
A program may use at most 64 MiB of HBM per device.

v0:
```python
import jax
import jax.numpy as jnp
import numpy as np
from jax import lax
from jax.experimental import pallas as pl
from jax.experimental.pallas import tpu as pltpu
from jax.sharding import Mesh
from jax.sharding import PartitionSpec as P


ZH, YW, YA, CORE, ZL, X = AXES = ("zh", "yw", "ya", "core", "zl", "x")
SIZES = (2, 2, 4, 2, 4, 4)
SEQ = (ZH, YW, YA, CORE)
Y = (YW, YA)
CHIPS = (ZH, YW, YA)
TAU = (2, 3, 1, 0)
HALF = 128


def delivery():
    def number(seq_chip, core, mp):
        return (seq_chip * 2 + core) * 16 + mp

    edges = []
    for seq_chip in range(16):
        for h in range(2):
            for mp in range(16):
                zeta, a = divmod(seq_chip, 4)
                z, x = divmod(mp, 4)
                row = 4 * z + a
                if zeta == z:
                    col, hc = 4 * z + x, (h if a >= x else 1 - h)
                elif zeta == z ^ 1:
                    col, hc = 4 * (z ^ 1) + x, (h if z % 2 else 1 - h)
                else:
                    col, hc = 4 * TAU[z] + x, (0 if zeta == z ^ 2 else 1)
                src = number(seq_chip, h, mp)
                if row == col:
                    continue
                edges.append((src, number(row, h, col), hc, 0))
                edges.append((src, number(col, hc, row), h, 1))
    by_src, by_dst = {}, {}
    for e, (s, d, _, _) in enumerate(edges):
        by_src.setdefault(s, []).append(e)
        by_dst.setdefault(d, []).append(e)
    colour = {}
    for first in range(len(edges)):
        e = first
        while e not in colour:
            colour[e] = 0
            s = edges[e][0]
            other = [k for k in by_src[s] if k != e][0]
            colour[other] = 1
            d = edges[other][1]
            e = [k for k in by_dst[d] if k != other][0]
    pairs = ([], [])
    table = np.zeros((512, 4), np.int32)
    for e, (s, d, half, turned) in enumerate(edges):
        k = colour[e]
        pairs[k].append((s, d))
        table[d, 2 * k] = turned
        table[d, 2 * k + 1] = half
    for mp in range(16):
        for h in range(2):
            own, other = number(mp, h, mp), number(mp, 1 - h, mp)
            pairs[1].append((own, other))
            table[own] = (0, h, h, 1 - h)
    return pairs, table


def around(x, axis, by):
    n = lax.axis_size(axis)
    return lax.ppermute(x, axis, [((i + by) % n, i) for i in range(n)])


def flipped(x, axis):
    n = lax.axis_size(axis)
    return lax.ppermute(x, axis, [(i, i ^ 1) for i in range(n)])


def products(where_ref, f0, f1, f2, f3, c1, ct, keep, send):
    x, z, core = where_ref[0], where_ref[1], where_ref[2]
    dims = (((0,), (0,)), ((), ()))
    for o, f in enumerate((f0, f1, f2, f3)):
        a = lax.rem(x + o, 4)

        def put(zeta, q0, q1):
            slot = zeta * 4 + a
            keep[slot] = jnp.where(core == 0, q0, q1)
            send[slot] = jnp.where(core == 0, q1, q0)

        lhs = f[...]
        for k, c in enumerate((f0, c1, ct)):
            p = lax.dot_general(lhs, c[...], dims, preferred_element_type=jnp.float32)
            p00, p01, p10, p11 = p[:HALF, :HALF], p[:HALF, HALF:], p[HALF:, :HALF], p[HALF:, HALF:]
            if k < 2:
                same = (a >= x) if k == 0 else (lax.rem(z, 2) == 1)
                put(z if k == 0 else z ^ 1, jnp.where(same, p00, p01), jnp.where(same, p11, p10))
            else:
                put(z ^ 2, p00, p10)
                put(z ^ 3, p01, p11)


def all_products(where, rows, c1, ct):
    shape = jax.ShapeDtypeStruct((16, HALF, HALF), jnp.float32)
    vmem = pl.BlockSpec(memory_space=pltpu.VMEM)
    return pl.pallas_call(
        products,
        out_shape=(shape, shape),
        in_specs=[pl.BlockSpec(memory_space=pltpu.SMEM)] + [vmem] * 6,
        out_specs=(vmem, vmem),
        compiler_params=pltpu.CompilerParams(vmem_limit_bytes=16 << 20),
        cost_estimate=pl.CostEstimate(flops=2 * 1024 * 1024 * 768, bytes_accessed=5 << 20, transcendentals=0),
        name="products",
    )(where, *rows, c1, ct)


def causal_conv(extended, weights, bias, position, doc_start, counted, length):
    taps = weights.shape[0]
    summed = jnp.zeros((length, weights.shape[1]), jnp.float32) + bias.astype(jnp.float32)
    for lag in range(taps):
        window = extended[taps - 1 - lag : taps - 1 - lag + length].astype(jnp.float32)
        usable = position - lag >= doc_start
        summed = summed + jnp.where(usable[:, None], weights[lag].astype(jnp.float32) * window, 0.0)
    return jnp.where(counted[:, None], jax.nn.silu(summed), 0.0).astype(jnp.bfloat16)


def on_device(inputs, conv_weight, conv_bias, doc_start, counts):
    pairs, table = delivery()
    length, width = inputs.shape
    taps = conv_weight.shape[0]
    core, z, x = lax.axis_index(CORE), lax.axis_index(ZL), lax.axis_index(X)
    chip = lax.axis_index(CHIPS)

    count = counts[0]
    tail = jnp.concatenate(
        [
            inputs[length - (taps - 1) :],
            jnp.full((1, width), (count // 32).astype(jnp.bfloat16)),
            jnp.full((1, width), (count % 32).astype(jnp.bfloat16)),
        ],
        axis=0,
    )
    shards = lax.axis_size(SEQ)
    prior = lax.ppermute(tail, SEQ, [(i, (i + 1) % shards) for i in range(shards)])
    count_pair = (
        count.astype(jnp.float32)
        + prior[taps - 1, 0].astype(jnp.float32) * 32.0
        + prior[taps, 0].astype(jnp.float32)
    )
    position = lax.axis_index(SEQ) * length + jnp.arange(length, dtype=jnp.int32)
    counted = jnp.arange(length, dtype=jnp.int32) < count
    extended = jnp.concatenate([prior[: taps - 1], inputs], axis=0)
    own = causal_conv(extended, conv_weight, conv_bias, position, doc_start, counted, length)

    ct = lax.ppermute(own, ZL, [(TAU[i], i) for i in range(4)])
    f1 = around(own, X, 1)
    f3 = around(own, X, 3)
    c1 = flipped(own, ZL)
    f2 = around(own, X, 2)

    corner = lax.dot_general(
        own[:, :HALF], own[:, HALF:], (((0,), (0,)), ((), ())), preferred_element_type=jnp.float32
    )
    goal = lax.rem(z, 2) * 4 + x
    pieces = jnp.where((jnp.arange(8, dtype=jnp.int32) == goal)[:, None, None], corner[None], 0.0)
    pieces = jnp.concatenate([pieces, jnp.full((8, 8, HALF), count_pair)], axis=1)
    early = lax.all_to_all(pieces, Y, split_axis=0, concat_axis=0, tiled=True)
    early = early.sum(axis=0)
    early = early + flipped(early, ZH)
    corner, total = early[:HALF], early[HALF, 0]

    where = jnp.stack([x, z, core]).astype(jnp.int32)
    f1, f2, f3, c1, ct, corner, total = lax.optimization_barrier((f1, f2, f3, c1, ct, corner, total))
    keep, send = all_products(where, (own, f1, f2, f3), c1, ct)
    mine = keep + flipped(send, CORE)
    quad = lax.all_to_all(mine, CHIPS, split_axis=0, concat_axis=0, tiled=True).sum(axis=0)

    diagonal = chip == 4 * z + x
    second = lax.optimization_barrier(jnp.where(diagonal, corner, quad))
    r1 = lax.ppermute(quad, AXES, pairs[0])
    r2 = lax.ppermute(second, AXES, pairs[1])
    r1, r2 = lax.optimization_barrier((r1, r2))
    me = jnp.asarray(table)[lax.axis_index(AXES)]
    r1 = jnp.where(diagonal, quad, r1)
    r2 = jnp.where(diagonal, corner + r2, r2)
    r1 = jnp.where(me[0] == 1, r1.T, r1)
    r2 = jnp.where(me[2] == 1, r2.T, r2)
    first = me[1] == 0
    summed = jnp.concatenate([jnp.where(first, r1, r2), jnp.where(first, r2, r1)], axis=1)
    return summed / total


def solution(mesh):
    torus = Mesh(mesh.devices.reshape(SIZES), AXES)
    mp = (ZL, X)
    placed = (P(SEQ, mp), P(None, mp), P(mp), P(SEQ), P(SEQ))

    return jax.shard_map(on_device, mesh=torus, in_specs=placed, out_specs=P(SEQ, mp), check_vma=False)
```

profile of v0, /device:TPU:66, one launch (start us, length us, event | category | flops | bytes accessed | tf_op | source)
XLA Modules:
  0.0 146.9 jit_solution(4472333970153147779)
XLA Ops:
  1.6 1.9 %collective-permute-start = (bf16[5,256]{1,0:T(8,128)(2,1)S(1)}, bf16[5,256]{1,0:T(8,128)(2,1)S(1)}, u32[]{:S(2)}, u32[]{:S(2)}) collective-permute-start(bf16[5,256]{1,0:T(8,128)(2,1)S(1)} %maximum_maximum_fusion), channel_id=1, source_target_pairs={{0,16},{16,32},{32,48},{48,64},{64,80},{80,96},{96,112},{112,128},... | collective-permute-start | bytes 7688 | tf_op jit(solution)/shard_map/ppermute | solution.py:145
  5.6 9.6 %collective-permute-done = bf16[5,256]{1,0:T(8,128)(2,1)S(1)} collective-permute-done((bf16[5,256]{1,0:T(8,128)(2,1)S(1)}, bf16[5,256]{1,0:T(8,128)(2,1)S(1)}, u32[]{:S(2)}, u32[]{:S(2)}) %collective-permute-start) | collective-permute-done | bytes 2592 | tf_op jit(solution)/shard_map/ppermute | solution.py:145
  15.3 3.8 %select_convert_fusion.f0 = bf16[1024,256]{1,0:T(8,128)(2,1)S(1)} fusion(bf16[1024,256]{1,0:T(8,128)(2,1)} %param.6, bf16[3,256]{1,0:T(4,128)(2,1)S(1)} %slice.75, f32[256]{0:T(256)S(1)} %bitcast.33, f32[256]{0:T(256)S(1)} %bitcast.34, f32[256]{0:T(256)S(1)} %bitcast.32, f32[256]{0:T(256)S(1)} %bitcast.31, f32[256]{0:T(256)S(1)} %convert_element_type.45, ...), kind=kLoop, calls=%fused_computation | loop fusion | flops 8126464 | bytes 1060352 | tf_op jit(solution)/shard_map/convert_element_type | solution.py:125
  21.4 20.7 %all_to_all.10 = f32[8,136,128]{2,1,0:T(8,128)S(1)} all-to-all(f32[8,136,128]{2,1,0:T(8,128)S(1)} %concatenate.14), channel_id=1, replica_groups=mesh['zh'=2,'yw'=2,'ya'=4,'core'=2,'zl'=4,'x'=4] {'yw','ya'}, dimensions={0} | all-to-all | bytes 1114112 | tf_op jit(solution)/shard_map/all_to_all | solution.py:168
  42.1 5.7 %collective-permute-start.6 = (f32[136,128]{1,0:T(8,128)S(1)}, f32[136,128]{1,0:T(8,128)S(1)}, u32[]{:S(2)}, u32[]{:S(2)}) collective-permute-start(f32[136,128]{1,0:T(8,128)S(1)} %reduce_sum.18), channel_id=1, source_target_pairs={{0,256},{256,0},{1,257},{257,1},{2,258},{258,2},{3,259},{259,3},{4... | collective-permute-start | bytes 208904 | tf_op jit(solution)/shard_map/ppermute | solution.py:78
  47.8 3.4 %collective-permute-start.5 = (bf16[1024,256]{1,0:T(8,128)(2,1)S(1)}, bf16[1024,256]{1,0:T(8,128)(2,1)S(1)}, u32[]{:S(2)}, u32[]{:S(2)}) collective-permute-start(bf16[1024,256]{1,0:T(8,128)(2,1)S(1)} %select_convert_fusion.f0), channel_id=1, source_target_pairs={{8,0},{12,4},{4,8},{0,12},{9,1},{13,5},{5,9},{1,13},{10,2},{14,6},... | collective-permute-start | bytes 1572872 | tf_op jit(solution)/shard_map/ppermute | solution.py:156
  51.2 4.3 %collective-permute-start.4 = (bf16[1024,256]{1,0:T(8,128)(2,1)S(1)}, bf16[1024,256]{1,0:T(8,128)(2,1)S(1)}, u32[]{:S(2)}, u32[]{:S(2)}) collective-permute-start(bf16[1024,256]{1,0:T(8,128)(2,1)S(1)} %select_convert_fusion.f0), channel_id=1, source_target_pairs={{0,4},{4,0},{8,12},{12,8},{1,5},{5,1},{9,13},{13,9},{2,6},{6,2},{1... | collective-permute-start | bytes 1572872 | tf_op jit(solution)/shard_map/ppermute | solution.py:78
  55.5 3.4 %collective-permute-start.3 = (bf16[1024,256]{1,0:T(8,128)(2,1)S(1)}, bf16[1024,256]{1,0:T(8,128)(2,1)S(1)}, u32[]{:S(2)}, u32[]{:S(2)}) collective-permute-start(bf16[1024,256]{1,0:T(8,128)(2,1)S(1)} %select_convert_fusion.f0), channel_id=1, source_target_pairs={{3,0},{0,1},{1,2},{2,3},{7,4},{4,5},{5,6},{6,7},{11,8},{8,9},{9,10... | collective-permute-start | bytes 1572872 | tf_op jit(solution)/shard_map/ppermute | solution.py:73
  58.9 3.0 %collective-permute-start.2 = (bf16[1024,256]{1,0:T(8,128)(2,1)S(1)}, bf16[1024,256]{1,0:T(8,128)(2,1)S(1)}, u32[]{:S(2)}, u32[]{:S(2)}) collective-permute-start(bf16[1024,256]{1,0:T(8,128)(2,1)S(1)} %select_convert_fusion.f0), channel_id=1, source_target_pairs={{2,0},{3,1},{0,2},{1,3},{6,4},{7,5},{4,6},{5,7},{10,8},{11,9},{8,1... | collective-permute-start | bytes 1572872 | tf_op jit(solution)/shard_map/ppermute | solution.py:73
  62.0 4.1 %collective-permute-start.1 = (bf16[1024,256]{1,0:T(8,128)(2,1)S(1)}, bf16[1024,256]{1,0:T(8,128)(2,1)S(1)}, u32[]{:S(2)}, u32[]{:S(2)}) collective-permute-start(bf16[1024,256]{1,0:T(8,128)(2,1)S(1)} %select_convert_fusion.f0), channel_id=1, source_target_pairs={{1,0},{2,1},{3,2},{0,3},{5,4},{6,5},{7,6},{4,7},{9,8},{10,9},{11,1... | collective-permute-start | bytes 1572872 | tf_op jit(solution)/shard_map/ppermute | solution.py:73
  66.7 5.7 %collective-permute-done.5.ct = bf16[1024,256]{1,0:T(8,128)(2,1)S(1)} collective-permute-done((bf16[1024,256]{1,0:T(8,128)(2,1)S(1)}, bf16[1024,256]{1,0:T(8,128)(2,1)S(1)}, u32[]{:S(2)}, u32[]{:S(2)}) %collective-permute-start.5) | collective-permute-done | bytes 524320 | tf_op jit(solution)/shard_map/ppermute | solution.py:156
  72.4 1.9 %collective-permute-done.4.c1 = bf16[1024,256]{1,0:T(8,128)(2,1)S(1)} collective-permute-done((bf16[1024,256]{1,0:T(8,128)(2,1)S(1)}, bf16[1024,256]{1,0:T(8,128)(2,1)S(1)}, u32[]{:S(2)}, u32[]{:S(2)}) %collective-permute-start.4) | collective-permute-done | bytes 524320 | tf_op jit(solution)/shard_map/ppermute | solution.py:78
  74.3 2.8 %collective-permute-done.2.f2 = bf16[1024,256]{1,0:T(8,128)(2,1)S(1)} collective-permute-done((bf16[1024,256]{1,0:T(8,128)(2,1)S(1)}, bf16[1024,256]{1,0:T(8,128)(2,1)S(1)}, u32[]{:S(2)}, u32[]{:S(2)}) %collective-permute-start.2) | collective-permute-done | bytes 524320 | tf_op jit(solution)/shard_map/ppermute | solution.py:73
  77.1 5.7 %collective-permute-done.1.f1 = bf16[1024,256]{1,0:T(8,128)(2,1)S(1)} collective-permute-done((bf16[1024,256]{1,0:T(8,128)(2,1)S(1)}, bf16[1024,256]{1,0:T(8,128)(2,1)S(1)}, u32[]{:S(2)}, u32[]{:S(2)}) %collective-permute-start.1) | collective-permute-done | bytes 524320 | tf_op jit(solution)/shard_map/ppermute | solution.py:73
  82.9 2.5 %products.1 = (f32[16,128,128]{2,1,0:T(8,128)S(1)}, f32[16,128,128]{2,1,0:T(8,128)S(1)}) custom-call(s32[3]{0:T(128)S(1)} %pad_add_fusion.where_ref, bf16[1024,256]{1,0:T(8,128)(2,1)S(1)} %select_convert_fusion.f0, bf16[1024,256]{1,0:T(8,128)(2,1)S(1)} %collective-permute-done.1.f1, bf16[1024,256]{1,0:T(8,128)(2,1)S(1)} %collective-permute-done.2.f2, ...), custom_call_target="tpu_custom_call" | custom-call | flops 1610612736 | bytes 5242880 | tf_op jit(solution)/shard_map/products/pallas_call | solution.py:107
  85.3 1.9 %collective-permute-start.7 = (f32[16,128,128]{2,1,0:T(8,128)S(1)}, f32[16,128,128]{2,1,0:T(8,128)S(1)}, u32[]{:S(2)}, u32[]{:S(2)}) collective-permute-start(f32[16,128,128]{2,1,0:T(8,128)S(1)} %get-tuple-element.22), channel_id=1, source_target_pairs={{0,16},{16,0},{1,17},{17,1},{2,18},{18,2},{3,19},{19,3},{4,20},{20... | collective-permute-start | bytes 3145736 | tf_op jit(solution)/shard_map/ppermute | solution.py:78
  87.2 2.6 %collective-permute-done.7 = f32[16,128,128]{2,1,0:T(8,128)S(1)} collective-permute-done((f32[16,128,128]{2,1,0:T(8,128)S(1)}, f32[16,128,128]{2,1,0:T(8,128)S(1)}, u32[]{:S(2)}, u32[]{:S(2)}) %collective-permute-start.7) | collective-permute-done | bytes 1048608 | tf_op jit(solution)/shard_map/ppermute | solution.py:78
  89.9 1.1 add.113
  91.0 6.4 %all-to-all-start.1 = ((f32[16,128,128]{2,1,0:T(8,128)}), f32[16,128,128]{2,1,0:T(8,128)S(1)}, u32[]{:S(2)}, u32[]{:S(2)}) async-start(f32[16,128,128]{2,1,0:T(8,128)} %add.113), calls=%async_computation.1 | async-start | bytes 2097152 | tf_op jit(solution)/shard_map/all_to_all | solution.py:177
  98.1 31.0 %all-to-all-done.1 = f32[16,128,128]{2,1,0:T(8,128)S(1)} async-done(((f32[16,128,128]{2,1,0:T(8,128)}), f32[16,128,128]{2,1,0:T(8,128)S(1)}, u32[]{:S(2)}, u32[]{:S(2)}) %all-to-all-start.1) | async-done | bytes 1048608 | tf_op jit(solution)/shard_map/all_to_all | solution.py:177
  129.1 6.3 %collective-permute-start.8 = (f32[128,128]{1,0:T(8,128)S(1)}, f32[128,128]{1,0:T(8,128)S(1)}, u32[]{:S(2)}, u32[]{:S(2)}) collective-permute-start(f32[128,128]{1,0:T(8,128)S(1)} %reduce_sum.19), channel_id=1, source_target_pairs={{1,1},{2,2},{3,3},{4,128},{5,129},{6,130},{7,131},{8,260},{9,261},... | collective-permute-start | bytes 196616 | tf_op jit(solution)/shard_map/ppermute | solution.py:181
  135.4 3.0 %collective-permute-start.9 = (f32[128,128]{1,0:T(8,128)S(1)}, f32[128,128]{1,0:T(8,128)S(1)}, u32[]{:S(2)}, u32[]{:S(2)}) collective-permute-start(f32[128,128]{1,0:T(8,128)S(1)} %broadcast_select_fusion.2), channel_id=1, source_target_pairs={{1,48},{2,80},{3,112},{4,4},{5,36},{6,68},{7,100},{8,136},{9,168},... | collective-permute-start | bytes 196616 | tf_op jit(solution)/shard_map/ppermute | solution.py:182
  140.9 4.4 %collective-permute-done.9 = f32[128,128]{1,0:T(8,128)S(1)} collective-permute-done((f32[128,128]{1,0:T(8,128)S(1)}, f32[128,128]{1,0:T(8,128)S(1)}, u32[]{:S(2)}, u32[]{:S(2)}) %collective-permute-start.9) | collective-permute-done | bytes 65568 | tf_op jit(solution)/shard_map/ppermute | solution.py:182
  145.6 1.3 maximum_divide_fusion
  (36 shorter events, 6.3 us)
Async XLA Ops:
  1.6 13.6 %collective-permute-start = (bf16[5,256]{1,0:T(8,128)(2,1)S(1)}, bf16[5,256]{1,0:T(8,128)(2,1)S(1)}, u32[]{:S(2)}, u32[]{:S(2)}) collective-permute-start(bf16[5,256]{1,0:T(8,128)(2,1)S(1)} %maximum_maximum_fusion), channel_id=1, source_target_pairs={{0,16},{16,32},{32,48},{48,64},{64,80},{80,96},{96,112},{112,128},... | collective-permute-start | bytes 7688 | tf_op jit(solution)/shard_map/ppermute | solution.py:145
  3.5 0.7 copy-start
  4.2 0.7 copy-start.1
  4.9 0.7 copy-start.2
  42.1 19.9 %collective-permute-start.6 = (f32[136,128]{1,0:T(8,128)S(1)}, f32[136,128]{1,0:T(8,128)S(1)}, u32[]{:S(2)}, u32[]{:S(2)}) collective-permute-start(f32[136,128]{1,0:T(8,128)S(1)} %reduce_sum.18), channel_id=1, source_target_pairs={{0,256},{256,0},{1,257},{257,1},{2,258},{258,2},{3,259},{259,3},{4... | collective-permute-start | bytes 208904 | tf_op jit(solution)/shard_map/ppermute | solution.py:78
  47.8 24.5 %collective-permute-start.5 = (bf16[1024,256]{1,0:T(8,128)(2,1)S(1)}, bf16[1024,256]{1,0:T(8,128)(2,1)S(1)}, u32[]{:S(2)}, u32[]{:S(2)}) collective-permute-start(bf16[1024,256]{1,0:T(8,128)(2,1)S(1)} %select_convert_fusion.f0), channel_id=1, source_target_pairs={{8,0},{12,4},{4,8},{0,12},{9,1},{13,5},{5,9},{1,13},{10,2},{14,6},... | collective-permute-start | bytes 1572872 | tf_op jit(solution)/shard_map/ppermute | solution.py:156
  51.2 23.0 %collective-permute-start.4 = (bf16[1024,256]{1,0:T(8,128)(2,1)S(1)}, bf16[1024,256]{1,0:T(8,128)(2,1)S(1)}, u32[]{:S(2)}, u32[]{:S(2)}) collective-permute-start(bf16[1024,256]{1,0:T(8,128)(2,1)S(1)} %select_convert_fusion.f0), channel_id=1, source_target_pairs={{0,4},{4,0},{8,12},{12,8},{1,5},{5,1},{9,13},{13,9},{2,6},{6,2},{1... | collective-permute-start | bytes 1572872 | tf_op jit(solution)/shard_map/ppermute | solution.py:78
  55.5 18.8 %collective-permute-start.3 = (bf16[1024,256]{1,0:T(8,128)(2,1)S(1)}, bf16[1024,256]{1,0:T(8,128)(2,1)S(1)}, u32[]{:S(2)}, u32[]{:S(2)}) collective-permute-start(bf16[1024,256]{1,0:T(8,128)(2,1)S(1)} %select_convert_fusion.f0), channel_id=1, source_target_pairs={{3,0},{0,1},{1,2},{2,3},{7,4},{4,5},{5,6},{6,7},{11,8},{8,9},{9,10... | collective-permute-start | bytes 1572872 | tf_op jit(solution)/shard_map/ppermute | solution.py:73
  58.9 18.2 %collective-permute-start.2 = (bf16[1024,256]{1,0:T(8,128)(2,1)S(1)}, bf16[1024,256]{1,0:T(8,128)(2,1)S(1)}, u32[]{:S(2)}, u32[]{:S(2)}) collective-permute-start(bf16[1024,256]{1,0:T(8,128)(2,1)S(1)} %select_convert_fusion.f0), channel_id=1, source_target_pairs={{2,0},{3,1},{0,2},{1,3},{6,4},{7,5},{4,6},{5,7},{10,8},{11,9},{8,1... | collective-permute-start | bytes 1572872 | tf_op jit(solution)/shard_map/ppermute | solution.py:73
  62.0 20.9 %collective-permute-start.1 = (bf16[1024,256]{1,0:T(8,128)(2,1)S(1)}, bf16[1024,256]{1,0:T(8,128)(2,1)S(1)}, u32[]{:S(2)}, u32[]{:S(2)}) collective-permute-start(bf16[1024,256]{1,0:T(8,128)(2,1)S(1)} %select_convert_fusion.f0), channel_id=1, source_target_pairs={{1,0},{2,1},{3,2},{0,3},{5,4},{6,5},{7,6},{4,7},{9,8},{10,9},{11,1... | collective-permute-start | bytes 1572872 | tf_op jit(solution)/shard_map/ppermute | solution.py:73
  85.3 4.6 %collective-permute-start.7 = (f32[16,128,128]{2,1,0:T(8,128)S(1)}, f32[16,128,128]{2,1,0:T(8,128)S(1)}, u32[]{:S(2)}, u32[]{:S(2)}) collective-permute-start(f32[16,128,128]{2,1,0:T(8,128)S(1)} %get-tuple-element.22), channel_id=1, source_target_pairs={{0,16},{16,0},{1,17},{17,1},{2,18},{18,2},{3,19},{19,3},{4,20},{20... | collective-permute-start | bytes 3145736 | tf_op jit(solution)/shard_map/ppermute | solution.py:78
  91.0 38.1 %all-to-all-start.1 = ((f32[16,128,128]{2,1,0:T(8,128)}), f32[16,128,128]{2,1,0:T(8,128)S(1)}, u32[]{:S(2)}, u32[]{:S(2)}) async-start(f32[16,128,128]{2,1,0:T(8,128)} %add.113), calls=%async_computation.1 | async-start | bytes 2097152 | tf_op jit(solution)/shard_map/all_to_all | solution.py:177
  129.1 16.2 %collective-permute-start.8 = (f32[128,128]{1,0:T(8,128)S(1)}, f32[128,128]{1,0:T(8,128)S(1)}, u32[]{:S(2)}, u32[]{:S(2)}) collective-permute-start(f32[128,128]{1,0:T(8,128)S(1)} %reduce_sum.19), channel_id=1, source_target_pairs={{1,1},{2,2},{3,3},{4,128},{5,129},{6,130},{7,131},{8,260},{9,261},... | collective-permute-start | bytes 196616 | tf_op jit(solution)/shard_map/ppermute | solution.py:181
  135.4 9.9 %collective-permute-start.9 = (f32[128,128]{1,0:T(8,128)S(1)}, f32[128,128]{1,0:T(8,128)S(1)}, u32[]{:S(2)}, u32[]{:S(2)}) collective-permute-start(f32[128,128]{1,0:T(8,128)S(1)} %broadcast_select_fusion.2), channel_id=1, source_target_pairs={{1,48},{2,80},{3,112},{4,4},{5,36},{6,68},{7,100},{8,136},{9,168},... | collective-permute-start | bytes 196616 | tf_op jit(solution)/shard_map/ppermute | solution.py:182
where the time goes:
time: 148 us; the launch traced here: 147 us
  waiting for transfers between devices  63.9 us (43%)
  starting transfers between devices  43.3 us (29%)
  blocking collectives  20.7 us (14%)
  other arithmetic  6.65 us (4%)
  local copies, waits for them, and re-layouts  5.56 us (4%)
  between operations  4.05 us (3%)
  Pallas kernels  2.46 us (2%)
    all_to_all x1, waiting for transfers between devices, on_device(): lax.all_to_all(mine, CHIPS, split_axis=0, concat_axis=0, tiled=True)  31 us
    all_to_all x1, blocking collectives, on_device(): early = lax.all_to_all(pieces, Y, split_axis=0, concat_axis=0, tiled=True)  20.7 us
    ppermute x3, starting transfers between devices, flipped(): return lax.ppermute(x, axis, [(i, i ^ 1) for i in range(n)])  11.9 us
    ppermute x3, starting transfers between devices, around(): return lax.ppermute(x, axis, [((i + by) % n, i) for i in range(n)])  10.5 us
    ppermute x1, waiting for transfers between devices, on_device(): lax.ppermute(tail, SEQ, [(i, (i + 1) % shards) for i in range(shards)])  9.65 us
    ppermute x3, waiting for transfers between devices, around(): return lax.ppermute(x, axis, [((i + by) % n, i) for i in range(n)])  8.58 us
    all_to_all x1, starting transfers between devices, on_device(): lax.all_to_all(mine, CHIPS, split_axis=0, concat_axis=0, tiled=True)  6.36 us
    ppermute x1, starting transfers between devices, on_device(): r1 = lax.ppermute(quad, AXES, pairs[0])  6.27 us
  transfers between devices with their start and end apart: 11, of which 8 were waited for; matrix products, arithmetic and copies ran while one was open for 1% of the time, Pallas kernels for 0%

commit v1 on v0

--- a/solution.py
+++ b/solution.py
@@ -11,7 +11,6 @@
 ZH, YW, YA, CORE, ZL, X = AXES = ("zh", "yw", "ya", "core", "zl", "x")
 SIZES = (2, 2, 4, 2, 4, 4)
 SEQ = (ZH, YW, YA, CORE)
-Y = (YW, YA)
 CHIPS = (ZH, YW, YA)
 TAU = (2, 3, 1, 0)
 HALF = 128
@@ -68,29 +67,23 @@
     return pairs, table
 
 
-def around(x, axis, by):
+def flipped(x, axis, bit=1):
     n = lax.axis_size(axis)
-    return lax.ppermute(x, axis, [((i + by) % n, i) for i in range(n)])
+    return lax.ppermute(x, axis, [(i, i ^ bit) for i in range(n)])
 
 
-def flipped(x, axis):
-    n = lax.axis_size(axis)
-    return lax.ppermute(x, axis, [(i, i ^ 1) for i in range(n)])
-
-
-def products(where_ref, f0, f1, f2, f3, c1, ct, keep, send):
+def products(where_ref, rows, own, c1, ct, keep, send):
     x, z, core = where_ref[0], where_ref[1], where_ref[2]
     dims = (((0,), (0,)), ((), ()))
-    for o, f in enumerate((f0, f1, f2, f3)):
-        a = lax.rem(x + o, 4)
+    for a in range(4):
 
         def put(zeta, q0, q1):
             slot = zeta * 4 + a
             keep[slot] = jnp.where(core == 0, q0, q1)
             send[slot] = jnp.where(core == 0, q1, q0)
 
-        lhs = f[...]
-        for k, c in enumerate((f0, c1, ct)):
+        lhs = rows[a]
+        for k, c in enumerate((own, c1, ct)):
             p = lax.dot_general(lhs, c[...], dims, preferred_element_type=jnp.float32)
             p00, p01, p10, p11 = p[:HALF, :HALF], p[:HALF, HALF:], p[HALF:, :HALF], p[HALF:, HALF:]
             if k < 2:
@@ -101,18 +94,18 @@
                 put(z ^ 3, p01, p11)
 
 
-def all_products(where, rows, c1, ct):
+def all_products(where, rows, own, c1, ct):
     shape = jax.ShapeDtypeStruct((16, HALF, HALF), jnp.float32)
     vmem = pl.BlockSpec(memory_space=pltpu.VMEM)
     return pl.pallas_call(
         products,
         out_shape=(shape, shape),
-        in_specs=[pl.BlockSpec(memory_space=pltpu.SMEM)] + [vmem] * 6,
+        in_specs=[pl.BlockSpec(memory_space=pltpu.SMEM)] + [vmem] * 4,
         out_specs=(vmem, vmem),
         compiler_params=pltpu.CompilerParams(vmem_limit_bytes=16 << 20),
         cost_estimate=pl.CostEstimate(flops=2 * 1024 * 1024 * 768, bytes_accessed=5 << 20, transcendentals=0),
         name="products",
-    )(where, *rows, c1, ct)
+    )(where, rows, own, c1, ct)
 
 
 def causal_conv(extended, weights, bias, position, doc_start, counted, length):
@@ -154,27 +147,26 @@
     own = causal_conv(extended, conv_weight, conv_bias, position, doc_start, counted, length)
 
     ct = lax.ppermute(own, ZL, [(TAU[i], i) for i in range(4)])
-    f1 = around(own, X, 1)
-    f3 = around(own, X, 3)
+    rows = lax.all_to_all(jnp.broadcast_to(own, (4, length, width)), X, split_axis=0, concat_axis=0, tiled=True)
     c1 = flipped(own, ZL)
-    f2 = around(own, X, 2)
 
     corner = lax.dot_general(
         own[:, :HALF], own[:, HALF:], (((0,), (0,)), ((), ())), preferred_element_type=jnp.float32
     )
-    goal = lax.rem(z, 2) * 4 + x
-    pieces = jnp.where((jnp.arange(8, dtype=jnp.int32) == goal)[:, None, None], corner[None], 0.0)
-    pieces = jnp.concatenate([pieces, jnp.full((8, 8, HALF), count_pair)], axis=1)
-    early = lax.all_to_all(pieces, Y, split_axis=0, concat_axis=0, tiled=True)
-    early = early.sum(axis=0)
-    early = early + flipped(early, ZH)
-    corner, total = early[:HALF], early[HALF, 0]
+    early = jnp.concatenate([corner, jnp.full((8, HALF), count_pair)], axis=0)
+    early = early + flipped(early, YA)
+    early = early + flipped(early, YA, 2)
+    early = early + flipped(early, YW)
+    rows, c1, ct, early = lax.optimization_barrier((rows, c1, ct, early))
 
     where = jnp.stack([x, z, core]).astype(jnp.int32)
-    f1, f2, f3, c1, ct, corner, total = lax.optimization_barrier((f1, f2, f3, c1, ct, corner, total))
-    keep, send = all_products(where, (own, f1, f2, f3), c1, ct)
+    keep, send = all_products(where, rows, own, c1, ct)
     mine = keep + flipped(send, CORE)
-    quad = lax.all_to_all(mine, CHIPS, split_axis=0, concat_axis=0, tiled=True).sum(axis=0)
+    quad = lax.all_to_all(mine, CHIPS, split_axis=0, concat_axis=0, tiled=True)
+    early = early + flipped(early, ZH)
+    quad, early = lax.optimization_barrier((quad, early))
+    quad = quad.sum(axis=0)
+    corner, total = early[:HALF], early[HALF, 0]
 
     diagonal = chip == 4 * z + x
     second = lax.optimization_barrier(jnp.where(diagonal, corner, quad))

time: 148 us -> 129 us (0.87)
  the two profiles are of different devices: /device:TPU:66 before, /device:TPU:70 now
where the time goes in v1:
time: 129 us; the launch traced here: 128 us
  waiting for transfers between devices  58.4 us (45%)
  starting transfers between devices  48.1 us (37%)
  other arithmetic  8.76 us (7%)
  local copies, waits for them, and re-layouts  5 us (4%)
  between operations  4.28 us (3%)
  Pallas kernels  2.93 us (2%)
    ppermute x6, waiting for transfers between devices, flipped(): return lax.ppermute(x, axis, [(i, i ^ bit) for i in range(n)])  41 us
    ppermute x6, starting transfers between devices, flipped(): return lax.ppermute(x, axis, [(i, i ^ bit) for i in range(n)])  19 us
    ppermute x1, starting transfers between devices, on_device(): r1 = lax.ppermute(quad, AXES, pairs[0])  10.4 us
    ppermute x1, waiting for transfers between devices, on_device(): lax.ppermute(tail, SEQ, [(i, (i + 1) % shards) for i in range(shards)])  9.51 us
    all_to_all x1, starting transfers between devices, on_device(): quad = lax.all_to_all(mine, CHIPS, split_axis=0, concat_axis=0, tiled=True)  6.91 us
    ppermute x1, waiting for transfers between devices, on_device(): r2 = lax.ppermute(second, AXES, pairs[1])  4.95 us
    all_to_all x1, starting transfers between devices, on_device(): lax.all_to_all(jnp.broadcast_to(own, (4, length, width)), X, split_axis=0...  4.77 us
    convert_element_type x1, other arithmetic, causal_conv(): jnp.where(counted[:, None], jax.nn.silu(summed), 0.0).astype(jnp.bfloat16)  3.8 us
  transfers between devices with their start and end apart: 12, of which 8 were waited for; matrix products, arithmetic and copies ran while one was open for 4% of the time, Pallas kernels for 0%

profile of v1, /device:TPU:70, one launch (start us, length us, event | category | flops | bytes accessed | tf_op | source)
XLA Modules:
  0.0 127.8 jit_solution(5413038543693519200)
XLA Ops:
  1.6 1.9 %collective-permute-start = (bf16[5,256]{1,0:T(8,128)(2,1)S(1)}, bf16[5,256]{1,0:T(8,128)(2,1)S(1)}, u32[]{:S(2)}, u32[]{:S(2)}) collective-permute-start(bf16[5,256]{1,0:T(8,128)(2,1)S(1)} %maximum_maximum_fusion), channel_id=1, source_target_pairs={{0,16},{16,32},{32,48},{48,64},{64,80},{80,96},{96,112},{112,128},... | collective-permute-start | bytes 7688 | tf_op jit(solution)/shard_map/ppermute | solution.py:138
  5.7 9.5 %collective-permute-done = bf16[5,256]{1,0:T(8,128)(2,1)S(1)} collective-permute-done((bf16[5,256]{1,0:T(8,128)(2,1)S(1)}, bf16[5,256]{1,0:T(8,128)(2,1)S(1)}, u32[]{:S(2)}, u32[]{:S(2)}) %collective-permute-start) | collective-permute-done | bytes 2592 | tf_op jit(solution)/shard_map/ppermute | solution.py:138
  15.3 3.8 %select_convert_fusion.own = bf16[1024,256]{1,0:T(8,128)(2,1)S(1)} fusion(bf16[1024,256]{1,0:T(8,128)(2,1)} %param.6, bf16[3,256]{1,0:T(4,128)(2,1)S(1)} %slice.75, f32[256]{0:T(256)S(1)} %bitcast.33, f32[256]{0:T(256)S(1)} %bitcast.34, f32[256]{0:T(256)S(1)} %bitcast.32, f32[256]{0:T(256)S(1)} %bitcast.31, f32[256]{0:T(256)S(1)} %convert_element_type.45, ...), kind=kLoop, calls=%fused_computation | loop fusion | flops 8126464 | bytes 1060352 | tf_op jit(solution)/shard_map/convert_element_type | solution.py:118
  19.1 1.5 %broadcast_in_dim.64 = bf16[4,1024,256]{2,1,0:T(8,128)(2,1)} broadcast(bf16[1024,256]{1,0:T(8,128)(2,1)S(1)} %select_convert_fusion.own), dimensions={1,2} | broadcast | bytes 2621440 | tf_op jit(solution)/shard_map/broadcast_in_dim | solution.py:150
  20.5 4.8 %all-to-all-start = ((bf16[4,1024,256]{2,1,0:T(8,128)(2,1)}), bf16[4,1024,256]{2,1,0:T(8,128)(2,1)S(1)}, u32[]{:S(2)}, u32[]{:S(2)}) async-start(bf16[4,1024,256]{2,1,0:T(8,128)(2,1)} %broadcast_in_dim.64), calls=%async_computation | async-start | bytes 4194304 | tf_op jit(solution)/shard_map/all_to_all | solution.py:150
  25.3 3.5 %collective-permute-start.1 = (bf16[1024,256]{1,0:T(8,128)(2,1)S(1)}, bf16[1024,256]{1,0:T(8,128)(2,1)S(1)}, u32[]{:S(2)}, u32[]{:S(2)}) collective-permute-start(bf16[1024,256]{1,0:T(8,128)(2,1)S(1)} %select_convert_fusion.own), channel_id=1, source_target_pairs={{0,4},{4,0},{8,12},{12,8},{1,5},{5,1},{9,13},{13,9},{2,6},{6,2},{1... | collective-permute-start | bytes 1572872 | tf_op jit(solution)/shard_map/ppermute | solution.py:72
  28.8 3.3 %collective-permute-start.2 = (bf16[1024,256]{1,0:T(8,128)(2,1)S(1)}, bf16[1024,256]{1,0:T(8,128)(2,1)}, u32[]{:S(2)}, u32[]{:S(2)}) collective-permute-start(bf16[1024,256]{1,0:T(8,128)(2,1)S(1)} %select_convert_fusion.own), channel_id=1, source_target_pairs={{8,0},{12,4},{4,8},{0,12},{9,1},{13,5},{5,9},{1,13},{10,2},{14,6},... | collective-permute-start | bytes 1572872 | tf_op jit(solution)/shard_map/ppermute | solution.py:149
  34.2 1.9 %collective-permute-start.3 = (f32[136,128]{1,0:T(8,128)S(1)}, f32[136,128]{1,0:T(8,128)S(1)}, u32[]{:S(2)}, u32[]{:S(2)}) collective-permute-start(f32[136,128]{1,0:T(8,128)S(1)} %concatenate.14), channel_id=1, source_target_pairs={{0,32},{32,0},{64,96},{96,64},{1,33},{33,1},{65,97},{97,65},{2,34}... | collective-permute-start | bytes 208904 | tf_op jit(solution)/shard_map/ppermute | solution.py:72
  36.1 4.8 %collective-permute-done.3 = f32[136,128]{1,0:T(8,128)S(1)} collective-permute-done((f32[136,128]{1,0:T(8,128)S(1)}, f32[136,128]{1,0:T(8,128)S(1)}, u32[]{:S(2)}, u32[]{:S(2)}) %collective-permute-start.3) | collective-permute-done | bytes 69664 | tf_op jit(solution)/shard_map/ppermute | solution.py:72
  40.9 1.9 %collective-permute-start.4 = (f32[136,128]{1,0:T(8,128)S(1)}, f32[136,128]{1,0:T(8,128)S(1)}, u32[]{:S(2)}, u32[]{:S(2)}) collective-permute-start(f32[136,128]{1,0:T(8,128)S(1)} %pad_add_fusion.1), channel_id=1, source_target_pairs={{0,64},{32,96},{64,0},{96,32},{1,65},{33,97},{65,1},{97,33},{2,66}... | collective-permute-start | bytes 208904 | tf_op jit(solution)/shard_map/ppermute | solution.py:72
  42.9 5.2 %collective-permute-done.4 = f32[136,128]{1,0:T(8,128)S(1)} collective-permute-done((f32[136,128]{1,0:T(8,128)S(1)}, f32[136,128]{1,0:T(8,128)S(1)}, u32[]{:S(2)}, u32[]{:S(2)}) %collective-permute-start.4) | collective-permute-done | bytes 69664 | tf_op jit(solution)/shard_map/ppermute | solution.py:72
  48.1 2.1 %collective-permute-start.5 = (f32[136,128]{1,0:T(8,128)S(1)}, f32[136,128]{1,0:T(8,128)S(1)}, u32[]{:S(2)}, u32[]{:S(2)}) collective-permute-start(f32[136,128]{1,0:T(8,128)S(1)} %add.118), channel_id=1, source_target_pairs={{0,128},{128,0},{1,129},{129,1},{2,130},{130,2},{3,131},{131,3},{4... | collective-permute-start | bytes 208904 | tf_op jit(solution)/shard_map/ppermute | solution.py:72
  50.2 8.0 %collective-permute-done.5 = f32[136,128]{1,0:T(8,128)S(1)} collective-permute-done((f32[136,128]{1,0:T(8,128)S(1)}, f32[136,128]{1,0:T(8,128)S(1)}, u32[]{:S(2)}, u32[]{:S(2)}) %collective-permute-start.5) | collective-permute-done | bytes 69664 | tf_op jit(solution)/shard_map/ppermute | solution.py:72
  58.2 2.9 %products.1 = (f32[16,128,128]{2,1,0:T(8,128)S(1)}, f32[16,128,128]{2,1,0:T(8,128)S(1)}) custom-call(s32[3]{0:T(128)S(1)} %pad_add_fusion.where_ref, bf16[4,1024,256]{2,1,0:T(8,128)(2,1)S(1)} %all-to-all-done.rows, bf16[1024,256]{1,0:T(8,128)(2,1)S(1)} %select_convert_fusion.own, bf16[1024,256]{1,0:T(8,128)(2,1)S(1)} %collective-permute-done.1.c1, ...), custom_call_target="tpu_custom_call" | custom-call | flops 1610612736 | bytes 5242880 | tf_op jit(solution)/shard_map/products/pallas_call | solution.py:100
  61.1 1.9 %collective-permute-start.6 = (f32[16,128,128]{2,1,0:T(8,128)S(1)}, f32[16,128,128]{2,1,0:T(8,128)S(1)}, u32[]{:S(2)}, u32[]{:S(2)}) collective-permute-start(f32[16,128,128]{2,1,0:T(8,128)S(1)} %get-tuple-element.19), channel_id=1, source_target_pairs={{0,16},{16,0},{1,17},{17,1},{2,18},{18,2},{3,19},{19,3},{4,20},{20... | collective-permute-start | bytes 3145736 | tf_op jit(solution)/shard_map/ppermute | solution.py:72
  63.1 2.6 %collective-permute-done.6 = f32[16,128,128]{2,1,0:T(8,128)S(1)} collective-permute-done((f32[16,128,128]{2,1,0:T(8,128)S(1)}, f32[16,128,128]{2,1,0:T(8,128)S(1)}, u32[]{:S(2)}, u32[]{:S(2)}) %collective-permute-start.6) | collective-permute-done | bytes 1048608 | tf_op jit(solution)/shard_map/ppermute | solution.py:72
  66.8 6.9 %all-to-all-start.1 = ((f32[16,128,128]{2,1,0:T(8,128)}), f32[16,128,128]{2,1,0:T(8,128)S(1)}, u32[]{:S(2)}, u32[]{:S(2)}) async-start(f32[16,128,128]{2,1,0:T(8,128)} %add.120), calls=%async_computation.1 | async-start | bytes 2097152 | tf_op jit(solution)/shard_map/all_to_all | solution.py:165
  73.8 7.7 %collective-permute-start.7 = (f32[136,128]{1,0:T(8,128)S(1)}, f32[136,128]{1,0:T(8,128)S(1)}, u32[]{:S(2)}, u32[]{:S(2)}) collective-permute-start(f32[136,128]{1,0:T(8,128)S(1)} %add.119), channel_id=1, source_target_pairs={{0,256},{256,0},{1,257},{257,1},{2,258},{258,2},{3,259},{259,3},{4... | collective-permute-start | bytes 208904 | tf_op jit(solution)/shard_map/ppermute | solution.py:72
  82.2 20.4 %collective-permute-done.7 = f32[136,128]{1,0:T(8,128)S(1)} collective-permute-done((f32[136,128]{1,0:T(8,128)S(1)}, f32[136,128]{1,0:T(8,128)S(1)}, u32[]{:S(2)}, u32[]{:S(2)}) %collective-permute-start.7) | collective-permute-done | bytes 69664 | tf_op jit(solution)/shard_map/ppermute | solution.py:72
  102.6 3.0 %all-to-all-done.1 = f32[16,128,128]{2,1,0:T(8,128)S(1)} async-done(((f32[16,128,128]{2,1,0:T(8,128)}), f32[16,128,128]{2,1,0:T(8,128)S(1)}, u32[]{:S(2)}, u32[]{:S(2)}) %all-to-all-start.1) | async-done | bytes 1048608 | tf_op jit(solution)/shard_map/all_to_all | solution.py:165
  105.6 10.4 %collective-permute-start.8 = (f32[128,128]{1,0:T(8,128)S(1)}, f32[128,128]{1,0:T(8,128)S(1)}, u32[]{:S(2)}, u32[]{:S(2)}) collective-permute-start(f32[128,128]{1,0:T(8,128)S(1)} %reduce_sum.9), channel_id=1, source_target_pairs={{1,1},{2,2},{3,3},{4,128},{5,129},{6,130},{7,131},{8,260},{9,261},... | collective-permute-start | bytes 196616 | tf_op jit(solution)/shard_map/ppermute | solution.py:173
  116.0 1.9 %collective-permute-start.9 = (f32[128,128]{1,0:T(8,128)S(1)}, f32[128,128]{1,0:T(8,128)S(1)}, u32[]{:S(2)}, u32[]{:S(2)}) collective-permute-start(f32[128,128]{1,0:T(8,128)S(1)} %slice_select_fusion), channel_id=1, source_target_pairs={{1,48},{2,80},{3,112},{4,4},{5,36},{6,68},{7,100},{8,136},{9,168},... | collective-permute-start | bytes 196616 | tf_op jit(solution)/shard_map/ppermute | solution.py:174
  121.2 4.9 %collective-permute-done.9 = f32[128,128]{1,0:T(8,128)S(1)} collective-permute-done((f32[128,128]{1,0:T(8,128)S(1)}, f32[128,128]{1,0:T(8,128)S(1)}, u32[]{:S(2)}, u32[]{:S(2)}) %collective-permute-start.9) | collective-permute-done | bytes 65568 | tf_op jit(solution)/shard_map/ppermute | solution.py:174
  126.4 1.4 %maximum_divide_fusion = f32[128,256]{1,0:T(8,128)} fusion(f32[128,128]{1,0:T(8,128)S(1)} %get-tuple-element.26, f32[128,128]{1,0:T(8,128)S(1)} %get-tuple-element.25, f32[]{:T(128)} %bitcast.15), kind=kLoop, calls=%fused_computation.9 | loop fusion | flops 65536 | bytes 262148 | tf_op jit(solution)/shard_map/div | solution.py:183
  (31 shorter events, 7.4 us)
Async XLA Ops:
  1.6 13.6 %collective-permute-start = (bf16[5,256]{1,0:T(8,128)(2,1)S(1)}, bf16[5,256]{1,0:T(8,128)(2,1)S(1)}, u32[]{:S(2)}, u32[]{:S(2)}) collective-permute-start(bf16[5,256]{1,0:T(8,128)(2,1)S(1)} %maximum_maximum_fusion), channel_id=1, source_target_pairs={{0,16},{16,32},{32,48},{48,64},{64,80},{80,96},{96,112},{112,128},... | collective-permute-start | bytes 7688 | tf_op jit(solution)/shard_map/ppermute | solution.py:138
  20.5 37.7 %all-to-all-start = ((bf16[4,1024,256]{2,1,0:T(8,128)(2,1)}), bf16[4,1024,256]{2,1,0:T(8,128)(2,1)S(1)}, u32[]{:S(2)}, u32[]{:S(2)}) async-start(bf16[4,1024,256]{2,1,0:T(8,128)(2,1)} %broadcast_in_dim.64), calls=%async_computation | async-start | bytes 4194304 | tf_op jit(solution)/shard_map/all_to_all | solution.py:150
  25.3 32.9 %collective-permute-start.1 = (bf16[1024,256]{1,0:T(8,128)(2,1)S(1)}, bf16[1024,256]{1,0:T(8,128)(2,1)S(1)}, u32[]{:S(2)}, u32[]{:S(2)}) collective-permute-start(bf16[1024,256]{1,0:T(8,128)(2,1)S(1)} %select_convert_fusion.own), channel_id=1, source_target_pairs={{0,4},{4,0},{8,12},{12,8},{1,5},{5,1},{9,13},{13,9},{2,6},{6,2},{1... | collective-permute-start | bytes 1572872 | tf_op jit(solution)/shard_map/ppermute | solution.py:72
  28.8 29.4 %collective-permute-start.2 = (bf16[1024,256]{1,0:T(8,128)(2,1)S(1)}, bf16[1024,256]{1,0:T(8,128)(2,1)}, u32[]{:S(2)}, u32[]{:S(2)}) collective-permute-start(bf16[1024,256]{1,0:T(8,128)(2,1)S(1)} %select_convert_fusion.own), channel_id=1, source_target_pairs={{8,0},{12,4},{4,8},{0,12},{9,1},{13,5},{5,9},{1,13},{10,2},{14,6},... | collective-permute-start | bytes 1572872 | tf_op jit(solution)/shard_map/ppermute | solution.py:149
  34.2 6.7 %collective-permute-start.3 = (f32[136,128]{1,0:T(8,128)S(1)}, f32[136,128]{1,0:T(8,128)S(1)}, u32[]{:S(2)}, u32[]{:S(2)}) collective-permute-start(f32[136,128]{1,0:T(8,128)S(1)} %concatenate.14), channel_id=1, source_target_pairs={{0,32},{32,0},{64,96},{96,64},{1,33},{33,1},{65,97},{97,65},{2,34}... | collective-permute-start | bytes 208904 | tf_op jit(solution)/shard_map/ppermute | solution.py:72
  40.9 7.1 %collective-permute-start.4 = (f32[136,128]{1,0:T(8,128)S(1)}, f32[136,128]{1,0:T(8,128)S(1)}, u32[]{:S(2)}, u32[]{:S(2)}) collective-permute-start(f32[136,128]{1,0:T(8,128)S(1)} %pad_add_fusion.1), channel_id=1, source_target_pairs={{0,64},{32,96},{64,0},{96,32},{1,65},{33,97},{65,1},{97,33},{2,66}... | collective-permute-start | bytes 208904 | tf_op jit(solution)/shard_map/ppermute | solution.py:72
  48.1 10.1 %collective-permute-start.5 = (f32[136,128]{1,0:T(8,128)S(1)}, f32[136,128]{1,0:T(8,128)S(1)}, u32[]{:S(2)}, u32[]{:S(2)}) collective-permute-start(f32[136,128]{1,0:T(8,128)S(1)} %add.118), channel_id=1, source_target_pairs={{0,128},{128,0},{1,129},{129,1},{2,130},{130,2},{3,131},{131,3},{4... | collective-permute-start | bytes 208904 | tf_op jit(solution)/shard_map/ppermute | solution.py:72
  61.1 4.6 %collective-permute-start.6 = (f32[16,128,128]{2,1,0:T(8,128)S(1)}, f32[16,128,128]{2,1,0:T(8,128)S(1)}, u32[]{:S(2)}, u32[]{:S(2)}) collective-permute-start(f32[16,128,128]{2,1,0:T(8,128)S(1)} %get-tuple-element.19), channel_id=1, source_target_pairs={{0,16},{16,0},{1,17},{17,1},{2,18},{18,2},{3,19},{19,3},{4,20},{20... | collective-permute-start | bytes 3145736 | tf_op jit(solution)/shard_map/ppermute | solution.py:72
  66.8 38.8 %all-to-all-start.1 = ((f32[16,128,128]{2,1,0:T(8,128)}), f32[16,128,128]{2,1,0:T(8,128)S(1)}, u32[]{:S(2)}, u32[]{:S(2)}) async-start(f32[16,128,128]{2,1,0:T(8,128)} %add.120), calls=%async_computation.1 | async-start | bytes 2097152 | tf_op jit(solution)/shard_map/all_to_all | solution.py:165
  73.8 28.8 %collective-permute-start.7 = (f32[136,128]{1,0:T(8,128)S(1)}, f32[136,128]{1,0:T(8,128)S(1)}, u32[]{:S(2)}, u32[]{:S(2)}) collective-permute-start(f32[136,128]{1,0:T(8,128)S(1)} %add.119), channel_id=1, source_target_pairs={{0,256},{256,0},{1,257},{257,1},{2,258},{258,2},{3,259},{259,3},{4... | collective-permute-start | bytes 208904 | tf_op jit(solution)/shard_map/ppermute | solution.py:72
  105.6 20.5 %collective-permute-start.8 = (f32[128,128]{1,0:T(8,128)S(1)}, f32[128,128]{1,0:T(8,128)S(1)}, u32[]{:S(2)}, u32[]{:S(2)}) collective-permute-start(f32[128,128]{1,0:T(8,128)S(1)} %reduce_sum.9), channel_id=1, source_target_pairs={{1,1},{2,2},{3,3},{4,128},{5,129},{6,130},{7,131},{8,260},{9,261},... | collective-permute-start | bytes 196616 | tf_op jit(solution)/shard_map/ppermute | solution.py:173
  116.0 10.2 %collective-permute-start.9 = (f32[128,128]{1,0:T(8,128)S(1)}, f32[128,128]{1,0:T(8,128)S(1)}, u32[]{:S(2)}, u32[]{:S(2)}) collective-permute-start(f32[128,128]{1,0:T(8,128)S(1)} %slice_select_fusion), channel_id=1, source_target_pairs={{1,48},{2,80},{3,112},{4,4},{5,36},{6,68},{7,100},{8,136},{9,168},... | collective-permute-start | bytes 196616 | tf_op jit(solution)/shard_map/ppermute | solution.py:174

commit v2 on v1

--- a/solution.py
+++ b/solution.py
@@ -14,6 +14,7 @@
 CHIPS = (ZH, YW, YA)
 TAU = (2, 3, 1, 0)
 HALF = 128
+EXTRA = 8
 
 
 def delivery():
@@ -58,12 +59,13 @@
         k = colour[e]
         pairs[k].append((s, d))
         table[d, 2 * k] = turned
-        table[d, 2 * k + 1] = half
+        if k == 0:
+            table[d, 1] = half
     for mp in range(16):
         for h in range(2):
             own, other = number(mp, h, mp), number(mp, 1 - h, mp)
             pairs[1].append((own, other))
-            table[own] = (0, h, h, 1 - h)
+            table[own] = (0, h, 0, 1)
     return pairs, table
 
 
@@ -73,29 +75,43 @@
 
 
 def products(where_ref, rows, own, c1, ct, keep, send):
-    x, z, core = where_ref[0], where_ref[1], where_ref[2]
+    x, z, core, count = where_ref[0], where_ref[1], where_ref[2], where_ref[3]
     dims = (((0,), (0,)), ((), ()))
+    r = lax.broadcasted_iota(jnp.int32, (HALF, HALF), 0)
+    c = lax.broadcasted_iota(jnp.int32, (HALF, HALF), 1)
+    extra_row = lax.broadcasted_iota(jnp.int32, (EXTRA, HALF), 0)
+    counted = jnp.where(extra_row == 1, count.astype(jnp.float32), 0.0)
     for a in range(4):
 
         def put(zeta, q0, q1):
             slot = zeta * 4 + a
-            keep[slot] = jnp.where(core == 0, q0, q1)
-            send[slot] = jnp.where(core == 0, q1, q0)
+            keep[slot, :HALF] = jnp.where(core == 0, q0, q1)
+            send[slot, :HALF] = jnp.where(core == 0, q1, q0)
+            keep[slot, HALF:] = counted
+            send[slot, HALF:] = counted
 
         lhs = rows[a]
-        for k, c in enumerate((own, c1, ct)):
-            p = lax.dot_general(lhs, c[...], dims, preferred_element_type=jnp.float32)
+        for k, block in enumerate((own, c1, ct)):
+            p = lax.dot_general(lhs, block[...], dims, preferred_element_type=jnp.float32)
             p00, p01, p10, p11 = p[:HALF, :HALF], p[:HALF, HALF:], p[HALF:, :HALF], p[HALF:, HALF:]
-            if k < 2:
-                same = (a >= x) if k == 0 else (lax.rem(z, 2) == 1)
-                put(z if k == 0 else z ^ 1, jnp.where(same, p00, p01), jnp.where(same, p11, p10))
+            if k == 0:
+                reach = jnp.where(a > x, HALF, jnp.where(a == x, 0, -HALF))
+                same = r - c <= reach
+                put(z, jnp.where(same, p00, p01), jnp.where(same, p11, p10))
+                middle = jnp.sum(jnp.where((r == c) & (a == x), p01, 0.0), axis=0, keepdims=True)
+                middle = jnp.where(extra_row == 0, middle, counted)
+                keep[z * 4 + a, HALF:] = middle
+                send[z * 4 + a, HALF:] = middle
+            elif k == 1:
+                same = lax.rem(z, 2) == 1
+                put(z ^ 1, jnp.where(same, p00, p01), jnp.where(same, p11, p10))
             else:
                 put(z ^ 2, p00, p10)
                 put(z ^ 3, p01, p11)
 
 
 def all_products(where, rows, own, c1, ct):
-    shape = jax.ShapeDtypeStruct((16, HALF, HALF), jnp.float32)
+    shape = jax.ShapeDtypeStruct((16, HALF + EXTRA, HALF), jnp.float32)
     vmem = pl.BlockSpec(memory_space=pltpu.VMEM)
     return pl.pallas_call(
         products,
@@ -108,6 +124,34 @@
     )(where, rows, own, c1, ct)
 
 
+def assemble(how, quad, extra, r1, r2, out):
+    turn1, half1, turn2, diagonal = how[0] == 1, how[1], how[2] == 1, how[3] == 1
+    r = lax.broadcasted_iota(jnp.int32, (HALF, HALF), 0)
+    c = lax.broadcasted_iota(jnp.int32, (HALF, HALF), 1)
+    m, got1, got2 = quad[...], r1[...], r2[...]
+    turned2 = got2.T
+    own = jnp.where(r <= c, m, m.T)
+    cross = jnp.where(r > c, m, jnp.where(r == c, extra[0:1], turned2))
+    q1 = jnp.where(diagonal, own, jnp.where(turn1, got1.T, got1))
+    q2 = jnp.where(diagonal, cross, jnp.where(turn2, turned2, got2))
+    total = extra[1:2]
+    out[:, :HALF] = jnp.where(half1 == 0, q1, q2) / total
+    out[:, HALF:] = jnp.where(half1 == 0, q2, q1) / total
+
+
+def assembled(how, quad, extra, r1, r2):
+    vmem = pl.BlockSpec(memory_space=pltpu.VMEM)
+    return pl.pallas_call(
+        assemble,
+        out_shape=jax.ShapeDtypeStruct((HALF, 2 * HALF), jnp.float32),
+        in_specs=[pl.BlockSpec(memory_space=pltpu.SMEM)] + [vmem] * 4,
+        out_specs=vmem,
+        compiler_params=pltpu.CompilerParams(vmem_limit_bytes=4 << 20),
+        cost_estimate=pl.CostEstimate(flops=1 << 20, bytes_accessed=1 << 19, transcendentals=0),
+        name="assemble",
+    )(how, quad, extra, r1, r2)
+
+
 def causal_conv(extended, weights, bias, position, doc_start, counted, length):
     taps = weights.shape[0]
     summed = jnp.zeros((length, weights.shape[1]), jnp.float32) + bias.astype(jnp.float32)
@@ -123,64 +167,29 @@
     length, width = inputs.shape
     taps = conv_weight.shape[0]
     core, z, x = lax.axis_index(CORE), lax.axis_index(ZL), lax.axis_index(X)
-    chip = lax.axis_index(CHIPS)
-
     count = counts[0]
-    tail = jnp.concatenate(
-        [
-            inputs[length - (taps - 1) :],
-            jnp.full((1, width), (count // 32).astype(jnp.bfloat16)),
-            jnp.full((1, width), (count % 32).astype(jnp.bfloat16)),
-        ],
-        axis=0,
-    )
+
     shards = lax.axis_size(SEQ)
-    prior = lax.ppermute(tail, SEQ, [(i, (i + 1) % shards) for i in range(shards)])
-    count_pair = (
-        count.astype(jnp.float32)
-        + prior[taps - 1, 0].astype(jnp.float32) * 32.0
-        + prior[taps, 0].astype(jnp.float32)
-    )
+    prior = lax.ppermute(inputs[length - (taps - 1) :], SEQ, [(i, (i + 1) % shards) for i in range(shards)])
     position = lax.axis_index(SEQ) * length + jnp.arange(length, dtype=jnp.int32)
     counted = jnp.arange(length, dtype=jnp.int32) < count
-    extended = jnp.concatenate([prior[: taps - 1], inputs], axis=0)
+    extended = jnp.concatenate([prior, inputs], axis=0)
     own = causal_conv(extended, conv_weight, conv_bias, position, doc_start, counted, length)
 
     ct = lax.ppermute(own, ZL, [(TAU[i], i) for i in range(4)])
     rows = lax.all_to_all(jnp.broadcast_to(own, (4, length, width)), X, split_axis=0, concat_axis=0, tiled=True)
     c1 = flipped(own, ZL)
 
-    corner = lax.dot_general(
-        own[:, :HALF], own[:, HALF:], (((0,), (0,)), ((), ())), preferred_element_type=jnp.float32
-    )
-    early = jnp.concatenate([corner, jnp.full((8, HALF), count_pair)], axis=0)
-    early = early + flipped(early, YA)
-    early = early + flipped(early, YA, 2)
-    early = early + flipped(early, YW)
-    rows, c1, ct, early = lax.optimization_barrier((rows, c1, ct, early))
-
-    where = jnp.stack([x, z, core]).astype(jnp.int32)
+    where = jnp.stack([x, z, core, count]).astype(jnp.int32)
     keep, send = all_products(where, rows, own, c1, ct)
     mine = keep + flipped(send, CORE)
-    quad = lax.all_to_all(mine, CHIPS, split_axis=0, concat_axis=0, tiled=True)
-    early = early + flipped(early, ZH)
-    quad, early = lax.optimization_barrier((quad, early))
-    quad = quad.sum(axis=0)
-    corner, total = early[:HALF], early[HALF, 0]
-
-    diagonal = chip == 4 * z + x
-    second = lax.optimization_barrier(jnp.where(diagonal, corner, quad))
+    summed = lax.all_to_all(mine, CHIPS, split_axis=0, concat_axis=0, tiled=True).sum(axis=0)
+    quad, extra = summed[:HALF], summed[HALF:]
+
     r1 = lax.ppermute(quad, AXES, pairs[0])
-    r2 = lax.ppermute(second, AXES, pairs[1])
-    r1, r2 = lax.optimization_barrier((r1, r2))
-    me = jnp.asarray(table)[lax.axis_index(AXES)]
-    r1 = jnp.where(diagonal, quad, r1)
-    r2 = jnp.where(diagonal, corner + r2, r2)
-    r1 = jnp.where(me[0] == 1, r1.T, r1)
-    r2 = jnp.where(me[2] == 1, r2.T, r2)
-    first = me[1] == 0
-    summed = jnp.concatenate([jnp.where(first, r1, r2), jnp.where(first, r2, r1)], axis=1)
-    return summed / total
+    r2 = lax.ppermute(quad, AXES, pairs[1])
+    how = lax.dynamic_index_in_dim(jnp.asarray(table), lax.axis_index(AXES), keepdims=False)
+    return assembled(how, quad, extra, r1, r2)
 
 
 def solution(mesh):

time: 129 us -> 123 us (0.953)
  the two profiles are of different devices: /device:TPU:70 before, /device:TPU:57 now
where the time goes in v2:
time: 123 us
  waiting for transfers between devices  59.7 us (49%)
  starting transfers between devices  47.8 us (39%)
  other arithmetic  7.24 us (6%)
  Pallas kernels  4.26 us (3%)
  local copies, waits for them, and re-layouts  2.87 us (2%)
    all_to_all x1, waiting for transfers between devices, on_device(): lax.all_to_all(mine, CHIPS, split_axis=0, concat_axis=0, tiled=True)  30.8 us
    ppermute x1, waiting for transfers between devices, on_device(): ct = lax.ppermute(own, ZL, [(TAU[i], i) for i in range(4)])  15.2 us
    all_to_all x1, starting transfers between devices, on_device(): lax.all_to_all(mine, CHIPS, split_axis=0, concat_axis=0, tiled=True)  12.4 us
    ppermute x1, starting transfers between devices, on_device(): lax.ppermute(inputs[length - (taps - 1):], SEQ, [(i, (i + 1) % shards) fo...  10.4 us
    ppermute x1, starting transfers between devices, on_device(): r2 = lax.ppermute(quad, AXES, pairs[1])  10.3 us
    ppermute x1, waiting for transfers between devices, on_device(): r1 = lax.ppermute(quad, AXES, pairs[0])  7.19 us
    ppermute x2, waiting for transfers between devices, flipped(): return lax.ppermute(x, axis, [(i, i ^ bit) for i in range(n)])  6.55 us
    ppermute x1, starting transfers between devices, on_device(): ct = lax.ppermute(own, ZL, [(TAU[i], i) for i in range(4)])  4.91 us
  transfers between devices with their start and end apart: 8, of which 5 were waited for; matrix products, arithmetic and copies ran while one was open for 2% of the time, Pallas kernels for 0%

profile of v2, /device:TPU:57, one launch (start us, length us, event | category | flops | bytes accessed | tf_op | source)
XLA Modules:
  0.0 122.5 jit_solution(14676798849164877307)
XLA Ops:
  0.0 0.7 slice.32
  0.7 10.4 %collective-permute-start = (bf16[3,256]{1,0:T(4,128)(2,1)S(1)}, bf16[3,256]{1,0:T(4,128)(2,1)S(1)}, u32[]{:S(2)}, u32[]{:S(2)}) collective-permute-start(bf16[3,256]{1,0:T(4,128)(2,1)S(1)} %slice.32), channel_id=1, source_target_pairs={{0,16},{16,32},{32,48},{48,64},{64,80},{80,96},{96,112},{112,128},... | collective-permute-start | bytes 4616 | tf_op jit(solution)/shard_map/ppermute | solution.py:173
  11.8 0.7 fusion.2
  12.5 0.8 slice_convert_fusion.3
  13.3 0.7 convert_element_type.26
  13.9 3.8 %select_convert_fusion.own = bf16[1024,256]{1,0:T(8,128)(2,1)S(1)} fusion(bf16[1024,256]{1,0:T(8,128)(2,1)} %param.6, bf16[3,256]{1,0:T(4,128)(2,1)S(1)} %collective-permute-done, f32[256]{0:T(256)S(1)} %bitcast.13, f32[256]{0:T(256)S(1)} %bitcast.14, f32[256]{0:T(256)S(1)} %bitcast.12, f32[256]{0:T(256)S(1)} %bitcast.11, f32[256]{0:T(256)S(1)} %convert_element_type.26, ...), kind=kLoop, calls=%fused_computation | loop fusion | flops 8126464 | bytes 1060352 | tf_op jit(solution)/shard_map/convert_element_type | solution.py:162
  17.8 1.5 %broadcast_in_dim.55 = bf16[4,1024,256]{2,1,0:T(8,128)(2,1)} broadcast(bf16[1024,256]{1,0:T(8,128)(2,1)S(1)} %select_convert_fusion.own), dimensions={1,2} | broadcast | bytes 2621440 | tf_op jit(solution)/shard_map/broadcast_in_dim | solution.py:180
  19.2 4.0 %all-to-all-start = ((bf16[4,1024,256]{2,1,0:T(8,128)(2,1)}), bf16[4,1024,256]{2,1,0:T(8,128)(2,1)S(1)}, u32[]{:S(2)}, u32[]{:S(2)}) async-start(bf16[4,1024,256]{2,1,0:T(8,128)(2,1)} %broadcast_in_dim.55), calls=%async_computation | async-start | bytes 4194304 | tf_op jit(solution)/shard_map/all_to_all | solution.py:180
  23.2 4.9 %collective-permute-start.2 = (bf16[1024,256]{1,0:T(8,128)(2,1)S(1)}, bf16[1024,256]{1,0:T(8,128)(2,1)S(1)}, u32[]{:S(2)}, u32[]{:S(2)}) collective-permute-start(bf16[1024,256]{1,0:T(8,128)(2,1)S(1)} %select_convert_fusion.own), channel_id=1, source_target_pairs={{8,0},{12,4},{4,8},{0,12},{9,1},{13,5},{5,9},{1,13},{10,2},{14,6},... | collective-permute-start | bytes 1572872 | tf_op jit(solution)/shard_map/ppermute | solution.py:179
  28.1 1.9 %collective-permute-start.1 = (bf16[1024,256]{1,0:T(8,128)(2,1)S(1)}, bf16[1024,256]{1,0:T(8,128)(2,1)}, u32[]{:S(2)}, u32[]{:S(2)}) collective-permute-start(bf16[1024,256]{1,0:T(8,128)(2,1)S(1)} %select_convert_fusion.own), channel_id=1, source_target_pairs={{0,4},{4,0},{8,12},{12,8},{1,5},{5,1},{9,13},{13,9},{2,6},{6,2},{1... | collective-permute-start | bytes 1572872 | tf_op jit(solution)/shard_map/ppermute | solution.py:74
  30.1 0.1 pad_add_fusion.where_ref
  30.2 15.2 %collective-permute-done.2.ct = bf16[1024,256]{1,0:T(8,128)(2,1)S(1)} collective-permute-done((bf16[1024,256]{1,0:T(8,128)(2,1)S(1)}, bf16[1024,256]{1,0:T(8,128)(2,1)S(1)}, u32[]{:S(2)}, u32[]{:S(2)}) %collective-permute-start.2) | collective-permute-done | bytes 524320 | tf_op jit(solution)/shard_map/ppermute | solution.py:179
  45.3 3.8 %collective-permute-done.1.c1 = bf16[1024,256]{1,0:T(8,128)(2,1)} collective-permute-done((bf16[1024,256]{1,0:T(8,128)(2,1)S(1)}, bf16[1024,256]{1,0:T(8,128)(2,1)}, u32[]{:S(2)}, u32[]{:S(2)}) %collective-permute-start.1) | collective-permute-done | bytes 524320 | tf_op jit(solution)/shard_map/ppermute | solution.py:74
  49.2 2.9 %products.1 = (f32[16,136,128]{2,1,0:T(8,128)S(1)}, f32[16,136,128]{2,1,0:T(8,128)S(1)}) custom-call(s32[4]{0:T(128)S(1)} %pad_add_fusion.where_ref, bf16[4,1024,256]{2,1,0:T(8,128)(2,1)S(1)} %all-to-all-done.rows, bf16[1024,256]{1,0:T(8,128)(2,1)S(1)} %select_convert_fusion.own, bf16[1024,256]{1,0:T(8,128)(2,1)} %collective-permute-done.1.c1, ...), custom_call_target="tpu_custom_call" | custom-call | flops 1610612736 | bytes 5242880 | tf_op jit(solution)/shard_map/products/pallas_call | solution.py:116
  52.1 1.9 %collective-permute-start.3 = (f32[16,136,128]{2,1,0:T(8,128)S(1)}, f32[16,136,128]{2,1,0:T(8,128)S(1)}, u32[]{:S(2)}, u32[]{:S(2)}) collective-permute-start(f32[16,136,128]{2,1,0:T(8,128)S(1)} %get-tuple-element.8), channel_id=1, source_target_pairs={{0,16},{16,0},{1,17},{17,1},{2,18},{18,2},{3,19},{19,3},{4,20},{20... | collective-permute-start | bytes 3342344 | tf_op jit(solution)/shard_map/ppermute | solution.py:74
  54.0 2.7 %collective-permute-done.3 = f32[16,136,128]{2,1,0:T(8,128)S(1)} collective-permute-done((f32[16,136,128]{2,1,0:T(8,128)S(1)}, f32[16,136,128]{2,1,0:T(8,128)S(1)}, u32[]{:S(2)}, u32[]{:S(2)}) %collective-permute-start.3) | collective-permute-done | bytes 1114144 | tf_op jit(solution)/shard_map/ppermute | solution.py:74
  56.7 1.1 add.78
  57.9 12.4 %all-to-all-start.1 = ((f32[16,136,128]{2,1,0:T(8,128)}), f32[16,136,128]{2,1,0:T(8,128)S(1)}, u32[]{:S(2)}, u32[]{:S(2)}) async-start(f32[16,136,128]{2,1,0:T(8,128)} %add.78), calls=%async_computation.1 | async-start | bytes 2228224 | tf_op jit(solution)/shard_map/all_to_all | solution.py:186
  70.3 30.8 %all-to-all-done.1 = f32[16,136,128]{2,1,0:T(8,128)S(1)} async-done(((f32[16,136,128]{2,1,0:T(8,128)}), f32[16,136,128]{2,1,0:T(8,128)S(1)}, u32[]{:S(2)}, u32[]{:S(2)}) %all-to-all-start.1) | async-done | bytes 1114144 | tf_op jit(solution)/shard_map/all_to_all | solution.py:186
  101.1 10.3 %collective-permute-start.5 = (f32[128,128]{1,0:T(8,128)S(1)}, f32[128,128]{1,0:T(8,128)S(1)}, u32[]{:S(2)}, u32[]{:S(2)}) collective-permute-start(f32[128,128]{1,0:T(8,128)S(1)} %slice.44.quad), channel_id=1, source_target_pairs={{1,48},{2,80},{3,112},{4,4},{5,36},{6,68},{7,100},{8,136},{9,168},... | collective-permute-start | bytes 196616 | tf_op jit(solution)/shard_map/ppermute | solution.py:190
  111.4 1.9 %collective-permute-start.4 = (f32[128,128]{1,0:T(8,128)S(1)}, f32[128,128]{1,0:T(8,128)S(1)}, u32[]{:S(2)}, u32[]{:S(2)}) collective-permute-start(f32[128,128]{1,0:T(8,128)S(1)} %slice.44.quad), channel_id=1, source_target_pairs={{1,1},{2,2},{3,3},{4,128},{5,129},{6,130},{7,131},{8,260},{9,261},... | collective-permute-start | bytes 196616 | tf_op jit(solution)/shard_map/ppermute | solution.py:189
  113.3 0.7 dynamic-slice_bitcast_fusion.how
  114.0 7.2 %collective-permute-done.4.r1 = f32[128,128]{1,0:T(8,128)S(1)} collective-permute-done((f32[128,128]{1,0:T(8,128)S(1)}, f32[128,128]{1,0:T(8,128)S(1)}, u32[]{:S(2)}, u32[]{:S(2)}) %collective-permute-start.4) | collective-permute-done | bytes 65568 | tf_op jit(solution)/shard_map/ppermute | solution.py:189
  121.2 1.3 %assemble.1 = f32[128,256]{1,0:T(8,128)} custom-call(s32[4]{0:T(128)S(1)} %dynamic-slice_bitcast_fusion.how, f32[128,128]{1,0:T(8,128)S(1)} %slice.44.quad, f32[8,128]{1,0:T(8,128)S(1)} %slice.45.extra, f32[128,128]{1,0:T(8,128)S(1)} %collective-permute-done.4.r1, f32[128,128]{1,0:T(8,128)S(1)} %collective-permute-done.5.r2), custom_call_target="tpu_custom_call" | custom-call | flops 1048576 | bytes 524288 | tf_op jit(solution)/shard_map/assemble/pallas_call | solution.py:144
  (6 shorter events, 0.1 us)
Async XLA Ops:
  0.7 13.3 %collective-permute-start = (bf16[3,256]{1,0:T(4,128)(2,1)S(1)}, bf16[3,256]{1,0:T(4,128)(2,1)S(1)}, u32[]{:S(2)}, u32[]{:S(2)}) collective-permute-start(bf16[3,256]{1,0:T(4,128)(2,1)S(1)} %slice.32), channel_id=1, source_target_pairs={{0,16},{16,32},{32,48},{48,64},{64,80},{80,96},{96,112},{112,128},... | collective-permute-start | bytes 4616 | tf_op jit(solution)/shard_map/ppermute | solution.py:173
  19.2 29.9 %all-to-all-start = ((bf16[4,1024,256]{2,1,0:T(8,128)(2,1)}), bf16[4,1024,256]{2,1,0:T(8,128)(2,1)S(1)}, u32[]{:S(2)}, u32[]{:S(2)}) async-start(bf16[4,1024,256]{2,1,0:T(8,128)(2,1)} %broadcast_in_dim.55), calls=%async_computation | async-start | bytes 4194304 | tf_op jit(solution)/shard_map/all_to_all | solution.py:180
  23.2 22.1 %collective-permute-start.2 = (bf16[1024,256]{1,0:T(8,128)(2,1)S(1)}, bf16[1024,256]{1,0:T(8,128)(2,1)S(1)}, u32[]{:S(2)}, u32[]{:S(2)}) collective-permute-start(bf16[1024,256]{1,0:T(8,128)(2,1)S(1)} %select_convert_fusion.own), channel_id=1, source_target_pairs={{8,0},{12,4},{4,8},{0,12},{9,1},{13,5},{5,9},{1,13},{10,2},{14,6},... | collective-permute-start | bytes 1572872 | tf_op jit(solution)/shard_map/ppermute | solution.py:179
  28.1 21.0 %collective-permute-start.1 = (bf16[1024,256]{1,0:T(8,128)(2,1)S(1)}, bf16[1024,256]{1,0:T(8,128)(2,1)}, u32[]{:S(2)}, u32[]{:S(2)}) collective-permute-start(bf16[1024,256]{1,0:T(8,128)(2,1)S(1)} %select_convert_fusion.own), channel_id=1, source_target_pairs={{0,4},{4,0},{8,12},{12,8},{1,5},{5,1},{9,13},{13,9},{2,6},{6,2},{1... | collective-permute-start | bytes 1572872 | tf_op jit(solution)/shard_map/ppermute | solution.py:74
  52.1 4.6 %collective-permute-start.3 = (f32[16,136,128]{2,1,0:T(8,128)S(1)}, f32[16,136,128]{2,1,0:T(8,128)S(1)}, u32[]{:S(2)}, u32[]{:S(2)}) collective-permute-start(f32[16,136,128]{2,1,0:T(8,128)S(1)} %get-tuple-element.8), channel_id=1, source_target_pairs={{0,16},{16,0},{1,17},{17,1},{2,18},{18,2},{3,19},{19,3},{4,20},{20... | collective-permute-start | bytes 3342344 | tf_op jit(solution)/shard_map/ppermute | solution.py:74
  57.9 43.2 %all-to-all-start.1 = ((f32[16,136,128]{2,1,0:T(8,128)}), f32[16,136,128]{2,1,0:T(8,128)S(1)}, u32[]{:S(2)}, u32[]{:S(2)}) async-start(f32[16,136,128]{2,1,0:T(8,128)} %add.78), calls=%async_computation.1 | async-start | bytes 2228224 | tf_op jit(solution)/shard_map/all_to_all | solution.py:186
  101.1 12.9 %collective-permute-start.5 = (f32[128,128]{1,0:T(8,128)S(1)}, f32[128,128]{1,0:T(8,128)S(1)}, u32[]{:S(2)}, u32[]{:S(2)}) collective-permute-start(f32[128,128]{1,0:T(8,128)S(1)} %slice.44.quad), channel_id=1, source_target_pairs={{1,48},{2,80},{3,112},{4,4},{5,36},{6,68},{7,100},{8,136},{9,168},... | collective-permute-start | bytes 196616 | tf_op jit(solution)/shard_map/ppermute | solution.py:190
  111.4 9.8 %collective-permute-start.4 = (f32[128,128]{1,0:T(8,128)S(1)}, f32[128,128]{1,0:T(8,128)S(1)}, u32[]{:S(2)}, u32[]{:S(2)}) collective-permute-start(f32[128,128]{1,0:T(8,128)S(1)} %slice.44.quad), channel_id=1, source_target_pairs={{1,1},{2,2},{3,3},{4,128},{5,129},{6,130},{7,131},{8,260},{9,261},... | collective-permute-start | bytes 196616 | tf_op jit(solution)/shard_map/ppermute | solution.py:189

commit v3 on v2

--- a/solution.py
+++ b/solution.py
@@ -152,32 +152,95 @@
     )(how, quad, extra, r1, r2)
 
 
-def causal_conv(extended, weights, bias, position, doc_start, counted, length):
-    taps = weights.shape[0]
-    summed = jnp.zeros((length, weights.shape[1]), jnp.float32) + bias.astype(jnp.float32)
-    for lag in range(taps):
-        window = extended[taps - 1 - lag : taps - 1 - lag + length].astype(jnp.float32)
-        usable = position - lag >= doc_start
-        summed = summed + jnp.where(usable[:, None], weights[lag].astype(jnp.float32) * window, 0.0)
-    return jnp.where(counted[:, None], jax.nn.silu(summed), 0.0).astype(jnp.bfloat16)
+def activated(window_of, code, weights, bias):
+    v = bias[...].astype(jnp.float32)
+    for lag in range(weights.shape[0]):
+        term = weights[lag : lag + 1, :].astype(jnp.float32) * window_of(lag)
+        v = v + jnp.where(code >= lag, term, 0.0)
+    return jnp.where(code >= 0, v * (1.0 / (1.0 + jnp.exp(-v))), 0.0)
+
+
+def codes(group, doc_start, counts):
+    token = group * HALF + lax.broadcasted_iota(jnp.int32, (1, HALF), 1)
+    place = lax.axis_index(SEQ) * (8 * HALF) + token
+    age = jnp.minimum(place - doc_start[group : group + 1, :], 3)
+    code = jnp.where(token < counts[0], age, -1).astype(jnp.float32)
+    column = jnp.broadcast_to(code, (HALF, HALF)).T
+    return jnp.concatenate([column, column], axis=1)
+
+
+def conv_body(counts, inputs, weights, bias, doc_start, out, lead):
+    lead[...] = inputs[:16, :]
+    for group in range(8):
+        base = group * HALF
+        code = codes(group, doc_start, counts)
+        if group:
+            wide = inputs[base - 16 : base + HALF, :].astype(jnp.float32)
+        else:
+            wide = jnp.concatenate([jnp.zeros((16, 2 * HALF), jnp.float32), inputs[:HALF, :].astype(jnp.float32)], axis=0)
+        value = activated(lambda lag: wide[16 - lag : 16 - lag + HALF], code, weights, bias)
+        out[base : base + HALF, :] = value.astype(jnp.bfloat16)
+
+
+def head_body(counts, main, lead, prior, weights, bias, doc_start, own, copies):
+    code = codes(0, doc_start, counts)[:16]
+    wide = jnp.concatenate([prior[...].astype(jnp.float32), lead[...].astype(jnp.float32)], axis=0)
+    value = activated(lambda lag: wide[8 - lag : 24 - lag], code, weights, bias)
+    head = value.astype(jnp.bfloat16)
+    rest = main[16:, :]
+    own[:16, :] = head
+    own[16:, :] = rest
+    for k in range(4):
+        copies[k, :16, :] = head
+        copies[k, 16:, :] = rest
+
+
+VMEM = pl.BlockSpec(memory_space=pltpu.VMEM)
+SMEM = pl.BlockSpec(memory_space=pltpu.SMEM)
+
+
+def conv_main(counts, inputs, weights, bias, doc_start):
+    return pl.pallas_call(
+        conv_body,
+        out_shape=(
+            jax.ShapeDtypeStruct(inputs.shape, jnp.bfloat16),
+            jax.ShapeDtypeStruct((16, inputs.shape[1]), jnp.bfloat16),
+        ),
+        in_specs=[SMEM] + [VMEM] * 4,
+        out_specs=(VMEM, VMEM),
+        compiler_params=pltpu.CompilerParams(vmem_limit_bytes=8 << 20),
+        cost_estimate=pl.CostEstimate(flops=8 << 20, bytes_accessed=1 << 20, transcendentals=1 << 19),
+        name="conv_main",
+    )(counts, inputs, weights, bias, doc_start)
+
+
+def conv_head(counts, main, lead, prior, weights, bias, doc_start):
+    shape = jax.ShapeDtypeStruct(main.shape, jnp.bfloat16)
+    return pl.pallas_call(
+        head_body,
+        out_shape=(shape, jax.ShapeDtypeStruct((4, *main.shape), jnp.bfloat16)),
+        in_specs=[SMEM] + [VMEM] * 6,
+        out_specs=(VMEM, VMEM),
+        compiler_params=pltpu.CompilerParams(vmem_limit_bytes=8 << 20),
+        cost_estimate=pl.CostEstimate(flops=1 << 20, bytes_accessed=1 << 20, transcendentals=0),
+        name="conv_head",
+    )(counts, main, lead, prior, weights, bias, doc_start)
 
 
 def on_device(inputs, conv_weight, conv_bias, doc_start, counts):
     pairs, table = delivery()
     length, width = inputs.shape
-    taps = conv_weight.shape[0]
     core, z, x = lax.axis_index(CORE), lax.axis_index(ZL), lax.axis_index(X)
     count = counts[0]
 
     shards = lax.axis_size(SEQ)
-    prior = lax.ppermute(inputs[length - (taps - 1) :], SEQ, [(i, (i + 1) % shards) for i in range(shards)])
-    position = lax.axis_index(SEQ) * length + jnp.arange(length, dtype=jnp.int32)
-    counted = jnp.arange(length, dtype=jnp.int32) < count
-    extended = jnp.concatenate([prior, inputs], axis=0)
-    own = causal_conv(extended, conv_weight, conv_bias, position, doc_start, counted, length)
+    prior = lax.ppermute(inputs[length - 8 :], SEQ, [(i, i + 1) for i in range(shards - 1)])
+    bias, starts = conv_bias.reshape(1, width), doc_start.reshape(8, HALF)
+    main, lead = conv_main(counts, inputs, conv_weight, bias, starts)
+    own, copies = conv_head(counts, main, lead, prior, conv_weight, bias, starts)
 
     ct = lax.ppermute(own, ZL, [(TAU[i], i) for i in range(4)])
-    rows = lax.all_to_all(jnp.broadcast_to(own, (4, length, width)), X, split_axis=0, concat_axis=0, tiled=True)
+    rows = lax.all_to_all(copies, X, split_axis=0, concat_axis=0, tiled=True)
     c1 = flipped(own, ZL)
 
     where = jnp.stack([x, z, core, count]).astype(jnp.int32)

time: 123 us -> 123 us (level)
  other arithmetic: 7.24 us -> 1.27 us
  local copies, waits for them, and re-layouts: 2.87 us -> 7.15 us
  Pallas kernels: 4.26 us -> 5.54 us
    unnamed x0 -> x12, local copies, waits for them, and re-layouts: none -> 5.09 us
    convert_element_type x2 -> x0, other arithmetic: 4.45 us -> none  [the longest x1 3.8 us: causal_conv(): jnp.where(counted[:, None], jax.nn.silu(summed), 0.0).astype(jnp.bfloat16)]
    broadcast_in_dim x1 -> x0, local copies, waits for them, and re-layouts: 1.47 us -> none  [on_device(): jnp.broadcast_to(own, (4, length, width))]
    pallas_call x0 -> x2, Pallas kernels: none -> 1.24 us  [the longest x1 1.05 us: conv_main(): pl.pallas_call(conv_body, out_shape=(jax.ShapeDtypeStruct(inputs.shape, j...]
  transfers between devices with their start and end apart: 8 -> 8, of which waited for: 5 -> 5; matrix products, arithmetic and copies ran while one was open for 2% -> 1% of each run, Pallas kernels for 0% -> 1%
where the time goes in v3:
time: 123 us; the launch traced here: 122 us
  waiting for transfers between devices  59.5 us (48%)
  starting transfers between devices  47.9 us (39%)
  local copies, waits for them, and re-layouts  7.15 us (6%)
  Pallas kernels  5.54 us (5%)
  other arithmetic  1.27 us (1%)
    all_to_all x1, waiting for transfers between devices, on_device(): lax.all_to_all(mine, CHIPS, split_axis=0, concat_axis=0, tiled=True)  30.8 us
    ppermute x1, waiting for transfers between devices, on_device(): ct = lax.ppermute(own, ZL, [(TAU[i], i) for i in range(4)])  15 us
    all_to_all x1, starting transfers between devices, on_device(): lax.all_to_all(mine, CHIPS, split_axis=0, concat_axis=0, tiled=True)  12.5 us
    ppermute x1, starting transfers between devices, on_device(): lax.ppermute(inputs[length - 8:], SEQ, [(i, i + 1) for i in range(shards...  10.4 us
    ppermute x1, starting transfers between devices, on_device(): r2 = lax.ppermute(quad, AXES, pairs[1])  10.3 us
    ppermute x1, waiting for transfers between devices, on_device(): r1 = lax.ppermute(quad, AXES, pairs[0])  7.18 us
    ppermute x2, waiting for transfers between devices, flipped(): return lax.ppermute(x, axis, [(i, i ^ bit) for i in range(n)])  6.55 us
    unnamed x12, local copies, waits for them, and re-layouts  5.09 us
  transfers between devices with their start and end apart: 8, of which 5 were waited for; matrix products, arithmetic and copies ran while one was open for 1% of the time, Pallas kernels for 1%

profile of v3, /device:TPU:57, one launch (start us, length us, event | category | flops | bytes accessed | tf_op | source)
XLA Modules:
  0.0 122.2 jit_solution(4682254431012862439)
XLA Ops:
  0.0 0.7 slice.9
  0.7 10.4 %collective-permute-start = (bf16[8,256]{1,0:T(8,128)(2,1)S(1)}, bf16[8,256]{1,0:T(8,128)(2,1)S(1)}, u32[]{:S(2)}, u32[]{:S(2)}) collective-permute-start(bf16[8,256]{1,0:T(8,128)(2,1)S(1)} %slice.9), channel_id=1, source_target_pairs={{0,16},{16,32},{32,48},{48,64},{64,80},{80,96},{96,112},{112,128},... | collective-permute-start | bytes 12296 | tf_op jit(solution)/shard_map/ppermute | solution.py:237
  12.4 0.7 copy-done.1
  13.1 0.7 copy-done.3
  13.8 1.0 copy-done.5
  14.8 1.1 conv_main.1
  16.6 0.7 copy-done.4
  17.5 1.3 %copy-done = bf16[4,1024,256]{2,1,0:T(8,128)(2,1)} copy-done((bf16[4,1024,256]{2,1,0:T(8,128)(2,1)}, bf16[4,1024,256]{2,1,0:T(8,128)(2,1)S(1)}, u32[]{:S(2)}) %copy-start) | copy-done | bytes 2097176
  18.8 4.0 %all-to-all-start = ((bf16[4,1024,256]{2,1,0:T(8,128)(2,1)}), bf16[4,1024,256]{2,1,0:T(8,128)(2,1)S(1)}, u32[]{:S(2)}, u32[]{:S(2)}) async-start(bf16[4,1024,256]{2,1,0:T(8,128)(2,1)} %copy-done), calls=%async_computation | async-start | bytes 4194304 | tf_op jit(solution)/shard_map/all_to_all | solution.py:243
  22.8 4.9 %collective-permute-start.2 = (bf16[1024,256]{1,0:T(8,128)(2,1)S(1)}, bf16[1024,256]{1,0:T(8,128)(2,1)S(1)}, u32[]{:S(2)}, u32[]{:S(2)}) collective-permute-start(bf16[1024,256]{1,0:T(8,128)(2,1)S(1)} %get-tuple-element.14.own), channel_id=1, source_target_pairs={{8,0},{12,4},{4,8},{0,12},{9,1},{13,5},{5,9},{1,13},{10,2},{14,6},... | collective-permute-start | bytes 1572872 | tf_op jit(solution)/shard_map/ppermute | solution.py:242
  27.7 1.9 %collective-permute-start.1 = (bf16[1024,256]{1,0:T(8,128)(2,1)S(1)}, bf16[1024,256]{1,0:T(8,128)(2,1)}, u32[]{:S(2)}, u32[]{:S(2)}) collective-permute-start(bf16[1024,256]{1,0:T(8,128)(2,1)S(1)} %get-tuple-element.14.own), channel_id=1, source_target_pairs={{0,4},{4,0},{8,12},{12,8},{1,5},{5,1},{9,13},{13,9},{2,6},{6,2},{1... | collective-permute-start | bytes 1572872 | tf_op jit(solution)/shard_map/ppermute | solution.py:74
  29.7 15.0 %collective-permute-done.2.ct = bf16[1024,256]{1,0:T(8,128)(2,1)S(1)} collective-permute-done((bf16[1024,256]{1,0:T(8,128)(2,1)S(1)}, bf16[1024,256]{1,0:T(8,128)(2,1)S(1)}, u32[]{:S(2)}, u32[]{:S(2)}) %collective-permute-start.2) | collective-permute-done | bytes 524320 | tf_op jit(solution)/shard_map/ppermute | solution.py:242
  44.8 3.8 %collective-permute-done.1.c1 = bf16[1024,256]{1,0:T(8,128)(2,1)} collective-permute-done((bf16[1024,256]{1,0:T(8,128)(2,1)S(1)}, bf16[1024,256]{1,0:T(8,128)(2,1)}, u32[]{:S(2)}, u32[]{:S(2)}) %collective-permute-start.1) | collective-permute-done | bytes 524320 | tf_op jit(solution)/shard_map/ppermute | solution.py:74
  48.6 3.0 %products.1 = (f32[16,136,128]{2,1,0:T(8,128)S(1)}, f32[16,136,128]{2,1,0:T(8,128)S(1)}) custom-call(s32[4]{0:T(128)S(1)} %pad_add_fusion.where_ref, bf16[4,1024,256]{2,1,0:T(8,128)(2,1)S(1)} %all-to-all-done.rows, bf16[1024,256]{1,0:T(8,128)(2,1)S(1)} %get-tuple-element.14.own, bf16[1024,256]{1,0:T(8,128)(2,1)} %collective-permute-done.1.c1, ...), custom_call_target="tpu_custom_call" | custom-call | flops 1610612736 | bytes 5242880 | tf_op jit(solution)/shard_map/products/pallas_call | solution.py:116
  51.6 1.9 %collective-permute-start.3 = (f32[16,136,128]{2,1,0:T(8,128)S(1)}, f32[16,136,128]{2,1,0:T(8,128)S(1)}, u32[]{:S(2)}, u32[]{:S(2)}) collective-permute-start(f32[16,136,128]{2,1,0:T(8,128)S(1)} %get-tuple-element.16), channel_id=1, source_target_pairs={{0,16},{16,0},{1,17},{17,1},{2,18},{18,2},{3,19},{19,3},{4,20},{20... | collective-permute-start | bytes 3342344 | tf_op jit(solution)/shard_map/ppermute | solution.py:74
  53.5 2.7 %collective-permute-done.3 = f32[16,136,128]{2,1,0:T(8,128)S(1)} collective-permute-done((f32[16,136,128]{2,1,0:T(8,128)S(1)}, f32[16,136,128]{2,1,0:T(8,128)S(1)}, u32[]{:S(2)}, u32[]{:S(2)}) %collective-permute-start.3) | collective-permute-done | bytes 1114144 | tf_op jit(solution)/shard_map/ppermute | solution.py:74
  56.2 1.1 add.28
  57.3 12.5 %all-to-all-start.1 = ((f32[16,136,128]{2,1,0:T(8,128)}), f32[16,136,128]{2,1,0:T(8,128)S(1)}, u32[]{:S(2)}, u32[]{:S(2)}) async-start(f32[16,136,128]{2,1,0:T(8,128)} %add.28), calls=%async_computation.1 | async-start | bytes 2228224 | tf_op jit(solution)/shard_map/all_to_all | solution.py:249
  69.9 30.8 %all-to-all-done.1 = f32[16,136,128]{2,1,0:T(8,128)S(1)} async-done(((f32[16,136,128]{2,1,0:T(8,128)}), f32[16,136,128]{2,1,0:T(8,128)S(1)}, u32[]{:S(2)}, u32[]{:S(2)}) %all-to-all-start.1) | async-done | bytes 1114144 | tf_op jit(solution)/shard_map/all_to_all | solution.py:249
  100.7 10.3 %collective-permute-start.5 = (f32[128,128]{1,0:T(8,128)S(1)}, f32[128,128]{1,0:T(8,128)S(1)}, u32[]{:S(2)}, u32[]{:S(2)}) collective-permute-start(f32[128,128]{1,0:T(8,128)S(1)} %slice.12.quad), channel_id=1, source_target_pairs={{1,48},{2,80},{3,112},{4,4},{5,36},{6,68},{7,100},{8,136},{9,168},... | collective-permute-start | bytes 196616 | tf_op jit(solution)/shard_map/ppermute | solution.py:253
  111.0 1.9 %collective-permute-start.4 = (f32[128,128]{1,0:T(8,128)S(1)}, f32[128,128]{1,0:T(8,128)S(1)}, u32[]{:S(2)}, u32[]{:S(2)}) collective-permute-start(f32[128,128]{1,0:T(8,128)S(1)} %slice.12.quad), channel_id=1, source_target_pairs={{1,1},{2,2},{3,3},{4,128},{5,129},{6,130},{7,131},{8,260},{9,261},... | collective-permute-start | bytes 196616 | tf_op jit(solution)/shard_map/ppermute | solution.py:252
  112.9 0.7 dynamic-slice_bitcast_fusion.how
  113.6 7.2 %collective-permute-done.4.r1 = f32[128,128]{1,0:T(8,128)S(1)} collective-permute-done((f32[128,128]{1,0:T(8,128)S(1)}, f32[128,128]{1,0:T(8,128)S(1)}, u32[]{:S(2)}, u32[]{:S(2)}) %collective-permute-start.4) | collective-permute-done | bytes 65568 | tf_op jit(solution)/shard_map/ppermute | solution.py:252
  120.8 1.3 %assemble.1 = f32[128,256]{1,0:T(8,128)} custom-call(s32[4]{0:T(128)S(1)} %dynamic-slice_bitcast_fusion.how, f32[128,128]{1,0:T(8,128)S(1)} %slice.12.quad, f32[8,128]{1,0:T(8,128)S(1)} %slice.13.extra, f32[128,128]{1,0:T(8,128)S(1)} %collective-permute-done.4.r1, f32[128,128]{1,0:T(8,128)S(1)} %collective-permute-done.5.r2), custom_call_target="tpu_custom_call" | custom-call | flops 1048576 | bytes 524288 | tf_op jit(solution)/shard_map/assemble/pallas_call | solution.py:144
  (16 shorter events, 1.7 us)
Async XLA Ops:
  0.7 15.2 %collective-permute-start = (bf16[8,256]{1,0:T(8,128)(2,1)S(1)}, bf16[8,256]{1,0:T(8,128)(2,1)S(1)}, u32[]{:S(2)}, u32[]{:S(2)}) collective-permute-start(bf16[8,256]{1,0:T(8,128)(2,1)S(1)} %slice.9), channel_id=1, source_target_pairs={{0,16},{16,32},{32,48},{48,64},{64,80},{80,96},{96,112},{112,128},... | collective-permute-start | bytes 12296 | tf_op jit(solution)/shard_map/ppermute | solution.py:237
  12.4 0.7 copy-start.1
  13.1 0.7 copy-start.3
  13.8 1.0 copy-start.5
  15.9 0.7 copy-start.2
  16.6 0.7 copy-start.4
  17.4 1.3 %copy-start = (bf16[4,1024,256]{2,1,0:T(8,128)(2,1)}, bf16[4,1024,256]{2,1,0:T(8,128)(2,1)S(1)}, u32[]{:S(2)}) copy-start(bf16[4,1024,256]{2,1,0:T(8,128)(2,1)S(1)} %get-tuple-element.13) | copy-start | bytes 6291460
  18.8 29.8 %all-to-all-start = ((bf16[4,1024,256]{2,1,0:T(8,128)(2,1)}), bf16[4,1024,256]{2,1,0:T(8,128)(2,1)S(1)}, u32[]{:S(2)}, u32[]{:S(2)}) async-start(bf16[4,1024,256]{2,1,0:T(8,128)(2,1)} %copy-done), calls=%async_computation | async-start | bytes 4194304 | tf_op jit(solution)/shard_map/all_to_all | solution.py:243
  22.8 22.0 %collective-permute-start.2 = (bf16[1024,256]{1,0:T(8,128)(2,1)S(1)}, bf16[1024,256]{1,0:T(8,128)(2,1)S(1)}, u32[]{:S(2)}, u32[]{:S(2)}) collective-permute-start(bf16[1024,256]{1,0:T(8,128)(2,1)S(1)} %get-tuple-element.14.own), channel_id=1, source_target_pairs={{8,0},{12,4},{4,8},{0,12},{9,1},{13,5},{5,9},{1,13},{10,2},{14,6},... | collective-permute-start | bytes 1572872 | tf_op jit(solution)/shard_map/ppermute | solution.py:242
  27.7 20.9 %collective-permute-start.1 = (bf16[1024,256]{1,0:T(8,128)(2,1)S(1)}, bf16[1024,256]{1,0:T(8,128)(2,1)}, u32[]{:S(2)}, u32[]{:S(2)}) collective-permute-start(bf16[1024,256]{1,0:T(8,128)(2,1)S(1)} %get-tuple-element.14.own), channel_id=1, source_target_pairs={{0,4},{4,0},{8,12},{12,8},{1,5},{5,1},{9,13},{13,9},{2,6},{6,2},{1... | collective-permute-start | bytes 1572872 | tf_op jit(solution)/shard_map/ppermute | solution.py:74
  51.6 4.6 %collective-permute-start.3 = (f32[16,136,128]{2,1,0:T(8,128)S(1)}, f32[16,136,128]{2,1,0:T(8,128)S(1)}, u32[]{:S(2)}, u32[]{:S(2)}) collective-permute-start(f32[16,136,128]{2,1,0:T(8,128)S(1)} %get-tuple-element.16), channel_id=1, source_target_pairs={{0,16},{16,0},{1,17},{17,1},{2,18},{18,2},{3,19},{19,3},{4,20},{20... | collective-permute-start | bytes 3342344 | tf_op jit(solution)/shard_map/ppermute | solution.py:74
  57.3 43.3 %all-to-all-start.1 = ((f32[16,136,128]{2,1,0:T(8,128)}), f32[16,136,128]{2,1,0:T(8,128)S(1)}, u32[]{:S(2)}, u32[]{:S(2)}) async-start(f32[16,136,128]{2,1,0:T(8,128)} %add.28), calls=%async_computation.1 | async-start | bytes 2228224 | tf_op jit(solution)/shard_map/all_to_all | solution.py:249
  100.7 12.9 %collective-permute-start.5 = (f32[128,128]{1,0:T(8,128)S(1)}, f32[128,128]{1,0:T(8,128)S(1)}, u32[]{:S(2)}, u32[]{:S(2)}) collective-permute-start(f32[128,128]{1,0:T(8,128)S(1)} %slice.12.quad), channel_id=1, source_target_pairs={{1,48},{2,80},{3,112},{4,4},{5,36},{6,68},{7,100},{8,136},{9,168},... | collective-permute-start | bytes 196616 | tf_op jit(solution)/shard_map/ppermute | solution.py:253
  111.0 9.8 %collective-permute-start.4 = (f32[128,128]{1,0:T(8,128)S(1)}, f32[128,128]{1,0:T(8,128)S(1)}, u32[]{:S(2)}, u32[]{:S(2)}) collective-permute-start(f32[128,128]{1,0:T(8,128)S(1)} %slice.12.quad), channel_id=1, source_target_pairs={{1,1},{2,2},{3,3},{4,128},{5,129},{6,130},{7,131},{8,260},{9,261},... | collective-permute-start | bytes 196616 | tf_op jit(solution)/shard_map/ppermute | solution.py:252

commit v4 on v3

--- a/solution.py
+++ b/solution.py
@@ -15,6 +15,10 @@
 TAU = (2, 3, 1, 0)
 HALF = 128
 EXTRA = 8
+PACK = 16
+LEVELS = 32767.0
+VMEM = pl.BlockSpec(memory_space=pltpu.VMEM)
+SMEM = pl.BlockSpec(memory_space=pltpu.SMEM)
 
 
 def delivery():
@@ -124,6 +128,74 @@
     )(where, rows, own, c1, ct)
 
 
+def scale_of(code):
+    return jnp.exp2(code * (1.0 / 256.0))
+
+
+def encode(keep, got, out):
+    row = lax.broadcasted_iota(jnp.int32, (PACK, HALF), 0)
+
+    def one(slot, carry):
+        v = keep[slot, :HALF] + got[slot, :HALF]
+        extra = keep[slot, HALF:] + got[slot, HALF:]
+        middle, count = extra[0:1], extra[1:2]
+        most = jnp.maximum(jnp.max(jnp.abs(v), axis=0, keepdims=True), jnp.abs(middle))
+        code = jnp.ceil(jnp.log2(jnp.maximum(most, 1e-37)) * 256.0)
+        rate = LEVELS / scale_of(code)
+        tail = jnp.where(row == 0, middle * rate, jnp.where(row == 1, code, jnp.where(row == 2, count, 0.0)))
+        out[slot, :HALF] = whole(v * rate)
+        out[slot, HALF:] = whole(tail)
+        return carry
+
+    lax.fori_loop(0, 16, one, 0)
+
+
+def whole(v):
+    return jnp.clip(jnp.round(v), -LEVELS, LEVELS).astype(jnp.int32).astype(jnp.int16)
+
+
+def decode(coded, quad, extra):
+    row = lax.broadcasted_iota(jnp.int32, (EXTRA, HALF), 0)
+
+    def one(slot, carry):
+        total, rest = carry
+        tail = coded[slot, HALF:].astype(jnp.int32).astype(jnp.float32)
+        scale = scale_of(tail[1:2]) * (1.0 / LEVELS)
+        total = total + coded[slot, :HALF].astype(jnp.int32).astype(jnp.float32) * scale
+        rest = rest + jnp.where(row == 0, tail[0:1] * scale, jnp.where(row == 1, tail[2:3], 0.0))
+        return total, rest
+
+    start = jnp.zeros((HALF, HALF), jnp.float32), jnp.zeros((EXTRA, HALF), jnp.float32)
+    quad[...], extra[...] = lax.fori_loop(0, 16, one, start)
+
+
+def encoded(keep, got):
+    return pl.pallas_call(
+        encode,
+        out_shape=jax.ShapeDtypeStruct((16, HALF + PACK, HALF), jnp.int16),
+        in_specs=[VMEM] * 2,
+        out_specs=VMEM,
+        compiler_params=pltpu.CompilerParams(vmem_limit_bytes=8 << 20),
+        cost_estimate=pl.CostEstimate(flops=2 << 20, bytes_accessed=3 << 20, transcendentals=0),
+        name="encode",
+    )(keep, got)
+
+
+def decoded(coded):
+    return pl.pallas_call(
+        decode,
+        out_shape=(
+            jax.ShapeDtypeStruct((HALF, HALF), jnp.float32),
+            jax.ShapeDtypeStruct((EXTRA, HALF), jnp.float32),
+        ),
+        in_specs=[VMEM],
+        out_specs=(VMEM, VMEM),
+        compiler_params=pltpu.CompilerParams(vmem_limit_bytes=8 << 20),
+        cost_estimate=pl.CostEstimate(flops=2 << 20, bytes_accessed=1 << 20, transcendentals=0),
+        name="decode",
+    )(coded)
+
+
 def assemble(how, quad, extra, r1, r2, out):
     turn1, half1, turn2, diagonal = how[0] == 1, how[1], how[2] == 1, how[3] == 1
     r = lax.broadcasted_iota(jnp.int32, (HALF, HALF), 0)
@@ -195,10 +267,6 @@
         copies[k, 16:, :] = rest
 
 
-VMEM = pl.BlockSpec(memory_space=pltpu.VMEM)
-SMEM = pl.BlockSpec(memory_space=pltpu.SMEM)
-
-
 def conv_main(counts, inputs, weights, bias, doc_start):
     return pl.pallas_call(
         conv_body,
@@ -245,9 +313,8 @@
 
     where = jnp.stack([x, z, core, count]).astype(jnp.int32)
     keep, send = all_products(where, rows, own, c1, ct)
-    mine = keep + flipped(send, CORE)
-    summed = lax.all_to_all(mine, CHIPS, split_axis=0, concat_axis=0, tiled=True).sum(axis=0)
-    quad, extra = summed[:HALF], summed[HALF:]
+    coded = encoded(keep, flipped(send, CORE))
+    quad, extra = decoded(lax.all_to_all(coded, CHIPS, split_axis=0, concat_axis=0, tiled=True))
 
     r1 = lax.ppermute(quad, AXES, pairs[0])
     r2 = lax.ppermute(quad, AXES, pairs[1])

time: 123 us -> 109 us (0.89)
  the two profiles are of different devices: /device:TPU:57 before, /device:TPU:56 now
where the time goes in v4:
time: 109 us; the launch traced here: 108 us
  waiting for transfers between devices  49.2 us (45%)
  starting transfers between devices  43.5 us (40%)
  Pallas kernels  7.55 us (7%)
  local copies, waits for them, and re-layouts  7.15 us (7%)
    all_to_all x1, waiting for transfers between devices, on_device(): lax.all_to_all(coded, CHIPS, split_axis=0, concat_axis=0, tiled=True)  20.3 us
    ppermute x1, waiting for transfers between devices, on_device(): ct = lax.ppermute(own, ZL, [(TAU[i], i) for i in range(4)])  18.4 us
    all_to_all x1, starting transfers between devices, on_device(): lax.all_to_all(coded, CHIPS, split_axis=0, concat_axis=0, tiled=True)  13.3 us
    ppermute x1, starting transfers between devices, on_device(): ct = lax.ppermute(own, ZL, [(TAU[i], i) for i in range(4)])  7.89 us
    ppermute x2, starting transfers between devices, flipped(): return lax.ppermute(x, axis, [(i, i ^ bit) for i in range(n)])  7 us
    ppermute x1, waiting for transfers between devices, on_device(): r1 = lax.ppermute(quad, AXES, pairs[0])  5.73 us
    unnamed x12, local copies, waits for them, and re-layouts  5.11 us
    ppermute x1, starting transfers between devices, on_device(): r1 = lax.ppermute(quad, AXES, pairs[0])  4.86 us
  transfers between devices with their start and end apart: 8, of which 5 were waited for; matrix products, arithmetic and copies ran while one was open for 1% of the time, Pallas kernels for 1%

profile of v4, /device:TPU:56, one launch (start us, length us, event | category | flops | bytes accessed | tf_op | source)
XLA Modules:
  0.0 108.3 jit_solution(12409823159866578482)
XLA Ops:
  0.0 0.7 slice.3
  0.7 1.9 %collective-permute-start = (bf16[8,256]{1,0:T(8,128)(2,1)S(1)}, bf16[8,256]{1,0:T(8,128)(2,1)S(1)}, u32[]{:S(2)}, u32[]{:S(2)}) collective-permute-start(bf16[8,256]{1,0:T(8,128)(2,1)S(1)} %slice.3), channel_id=1, source_target_pairs={{0,16},{16,32},{32,48},{48,64},{64,80},{80,96},{96,112},{112,128},... | collective-permute-start | bytes 12296 | tf_op jit(solution)/shard_map/ppermute | solution.py:305
  3.9 0.7 copy-done.1
  4.6 0.7 copy-done.3
  5.3 1.0 copy-done.5
  6.3 1.1 conv_main.1
  8.1 0.7 copy-done.4
  9.0 1.3 %copy-done = bf16[4,1024,256]{2,1,0:T(8,128)(2,1)} copy-done((bf16[4,1024,256]{2,1,0:T(8,128)(2,1)}, bf16[4,1024,256]{2,1,0:T(8,128)(2,1)S(1)}, u32[]{:S(2)}) %copy-start) | copy-done | bytes 2097176
  10.3 4.3 %all-to-all-start = ((bf16[4,1024,256]{2,1,0:T(8,128)(2,1)}), bf16[4,1024,256]{2,1,0:T(8,128)(2,1)S(1)}, u32[]{:S(2)}, u32[]{:S(2)}) async-start(bf16[4,1024,256]{2,1,0:T(8,128)(2,1)} %copy-done), calls=%async_computation | async-start | bytes 4194304 | tf_op jit(solution)/shard_map/all_to_all | solution.py:311
  14.6 7.9 %collective-permute-start.2 = (bf16[1024,256]{1,0:T(8,128)(2,1)S(1)}, bf16[1024,256]{1,0:T(8,128)(2,1)S(1)}, u32[]{:S(2)}, u32[]{:S(2)}) collective-permute-start(bf16[1024,256]{1,0:T(8,128)(2,1)S(1)} %get-tuple-element.16.own), channel_id=1, source_target_pairs={{8,0},{12,4},{4,8},{0,12},{9,1},{13,5},{5,9},{1,13},{10,2},{14,6},... | collective-permute-start | bytes 1572872 | tf_op jit(solution)/shard_map/ppermute | solution.py:310
  22.5 1.9 %collective-permute-start.1 = (bf16[1024,256]{1,0:T(8,128)(2,1)S(1)}, bf16[1024,256]{1,0:T(8,128)(2,1)}, u32[]{:S(2)}, u32[]{:S(2)}) collective-permute-start(bf16[1024,256]{1,0:T(8,128)(2,1)S(1)} %get-tuple-element.16.own), channel_id=1, source_target_pairs={{0,4},{4,0},{8,12},{12,8},{1,5},{5,1},{9,13},{13,9},{2,6},{6,2},{1... | collective-permute-start | bytes 1572872 | tf_op jit(solution)/shard_map/ppermute | solution.py:78
  24.5 18.4 %collective-permute-done.2.ct = bf16[1024,256]{1,0:T(8,128)(2,1)S(1)} collective-permute-done((bf16[1024,256]{1,0:T(8,128)(2,1)S(1)}, bf16[1024,256]{1,0:T(8,128)(2,1)S(1)}, u32[]{:S(2)}, u32[]{:S(2)}) %collective-permute-start.2) | collective-permute-done | bytes 524320 | tf_op jit(solution)/shard_map/ppermute | solution.py:310
  42.9 2.4 %collective-permute-done.1.c1 = bf16[1024,256]{1,0:T(8,128)(2,1)} collective-permute-done((bf16[1024,256]{1,0:T(8,128)(2,1)S(1)}, bf16[1024,256]{1,0:T(8,128)(2,1)}, u32[]{:S(2)}, u32[]{:S(2)}) %collective-permute-start.1) | collective-permute-done | bytes 524320 | tf_op jit(solution)/shard_map/ppermute | solution.py:78
  45.3 3.0 %products.1 = (f32[16,136,128]{2,1,0:T(8,128)S(1)}, f32[16,136,128]{2,1,0:T(8,128)S(1)}) custom-call(s32[4]{0:T(128)S(1)} %pad_add_fusion.where_ref, bf16[4,1024,256]{2,1,0:T(8,128)(2,1)S(1)} %all-to-all-done.rows, bf16[1024,256]{1,0:T(8,128)(2,1)S(1)} %get-tuple-element.16.own, bf16[1024,256]{1,0:T(8,128)(2,1)} %collective-permute-done.1.c1, ...), custom_call_target="tpu_custom_call" | custom-call | flops 1610612736 | bytes 5242880 | tf_op jit(solution)/shard_map/products/pallas_call | solution.py:120
  48.2 5.1 %collective-permute-start.3 = (f32[16,136,128]{2,1,0:T(8,128)S(1)}, f32[16,136,128]{2,1,0:T(8,128)S(1)}, u32[]{:S(2)}, u32[]{:S(2)}) collective-permute-start(f32[16,136,128]{2,1,0:T(8,128)S(1)} %get-tuple-element.18), channel_id=1, source_target_pairs={{0,16},{16,0},{1,17},{17,1},{2,18},{18,2},{3,19},{19,3},{4,20},{20... | collective-permute-start | bytes 3342344 | tf_op jit(solution)/shard_map/ppermute | solution.py:78
  53.3 2.4 %collective-permute-done.3.got = f32[16,136,128]{2,1,0:T(8,128)S(1)} collective-permute-done((f32[16,136,128]{2,1,0:T(8,128)S(1)}, f32[16,136,128]{2,1,0:T(8,128)S(1)}, u32[]{:S(2)}, u32[]{:S(2)}) %collective-permute-start.3) | collective-permute-done | bytes 1114144 | tf_op jit(solution)/shard_map/ppermute | solution.py:78
  55.7 1.7 %encode.1 = s16[16,144,128]{2,1,0:T(8,128)(2,1)} custom-call(f32[16,136,128]{2,1,0:T(8,128)S(1)} %get-tuple-element.17.keep, f32[16,136,128]{2,1,0:T(8,128)S(1)} %collective-permute-done.3.got), custom_call_target="tpu_custom_call" | custom-call | flops 2097152 | bytes 3145728 | tf_op jit(solution)/shard_map/encode/pallas_call | solution.py:173
  57.4 13.3 %all-to-all-start.1 = ((s16[16,144,128]{2,1,0:T(8,128)(2,1)}), s16[16,144,128]{2,1,0:T(8,128)(2,1)S(1)}, u32[]{:S(2)}, u32[]{:S(2)}) async-start(s16[16,144,128]{2,1,0:T(8,128)(2,1)} %encode.1), calls=%async_computation.1 | async-start | bytes 1179648 | tf_op jit(solution)/shard_map/all_to_all | solution.py:317
  70.7 20.3 %all-to-all-done.1.coded = s16[16,144,128]{2,1,0:T(8,128)(2,1)S(1)} async-done(((s16[16,144,128]{2,1,0:T(8,128)(2,1)}), s16[16,144,128]{2,1,0:T(8,128)(2,1)S(1)}, u32[]{:S(2)}, u32[]{:S(2)}) %all-to-all-start.1) | async-done | bytes 589856 | tf_op jit(solution)/shard_map/all_to_all | solution.py:317
  91.4 4.2 %collective-permute-start.5 = (f32[128,128]{1,0:T(8,128)S(1)}, f32[128,128]{1,0:T(8,128)S(1)}, u32[]{:S(2)}, u32[]{:S(2)}) collective-permute-start(f32[128,128]{1,0:T(8,128)S(1)} %get-tuple-element.19.quad), channel_id=1, source_target_pairs={{1,48},{2,80},{3,112},{4,4},{5,36},{6,68},{7,100},{8,136},{9,168},... | collective-permute-start | bytes 196616 | tf_op jit(solution)/shard_map/ppermute | solution.py:320
  95.7 4.9 %collective-permute-start.4 = (f32[128,128]{1,0:T(8,128)S(1)}, f32[128,128]{1,0:T(8,128)S(1)}, u32[]{:S(2)}, u32[]{:S(2)}) collective-permute-start(f32[128,128]{1,0:T(8,128)S(1)} %get-tuple-element.19.quad), channel_id=1, source_target_pairs={{1,1},{2,2},{3,3},{4,128},{5,129},{6,130},{7,131},{8,260},{9,261},... | collective-permute-start | bytes 196616 | tf_op jit(solution)/shard_map/ppermute | solution.py:319
  100.5 0.7 dynamic-slice_bitcast_fusion.how
  101.2 5.7 %collective-permute-done.4.r1 = f32[128,128]{1,0:T(8,128)S(1)} collective-permute-done((f32[128,128]{1,0:T(8,128)S(1)}, f32[128,128]{1,0:T(8,128)S(1)}, u32[]{:S(2)}, u32[]{:S(2)}) %collective-permute-start.4) | collective-permute-done | bytes 65568 | tf_op jit(solution)/shard_map/ppermute | solution.py:319
  107.0 1.3 %assemble.1 = f32[128,256]{1,0:T(8,128)} custom-call(s32[4]{0:T(128)S(1)} %dynamic-slice_bitcast_fusion.how, f32[128,128]{1,0:T(8,128)S(1)} %get-tuple-element.19.quad, f32[8,128]{1,0:T(8,128)S(1)} %get-tuple-element.20.extra, f32[128,128]{1,0:T(8,128)S(1)} %collective-permute-done.4.r1, f32[128,128]{1,0:T(8,128)S(1)} %collective-permute-done.5.r2), custom_call_target="tpu_custom_call" | custom-call | flops 1048576 | bytes 524288 | tf_op jit(solution)/shard_map/assemble/pallas_call | solution.py:216
  (14 shorter events, 2.0 us)
Async XLA Ops:
  0.7 6.7 %collective-permute-start = (bf16[8,256]{1,0:T(8,128)(2,1)S(1)}, bf16[8,256]{1,0:T(8,128)(2,1)S(1)}, u32[]{:S(2)}, u32[]{:S(2)}) collective-permute-start(bf16[8,256]{1,0:T(8,128)(2,1)S(1)} %slice.3), channel_id=1, source_target_pairs={{0,16},{16,32},{32,48},{48,64},{64,80},{80,96},{96,112},{112,128},... | collective-permute-start | bytes 12296 | tf_op jit(solution)/shard_map/ppermute | solution.py:305
  3.9 0.7 copy-start.1
  4.6 0.7 copy-start.3
  5.3 1.0 copy-start.5
  7.4 0.7 copy-start.2
  8.1 0.7 copy-start.4
  9.0 1.3 %copy-start = (bf16[4,1024,256]{2,1,0:T(8,128)(2,1)}, bf16[4,1024,256]{2,1,0:T(8,128)(2,1)S(1)}, u32[]{:S(2)}) copy-start(bf16[4,1024,256]{2,1,0:T(8,128)(2,1)S(1)} %get-tuple-element.15) | copy-start | bytes 6291460
  10.3 35.0 %all-to-all-start = ((bf16[4,1024,256]{2,1,0:T(8,128)(2,1)}), bf16[4,1024,256]{2,1,0:T(8,128)(2,1)S(1)}, u32[]{:S(2)}, u32[]{:S(2)}) async-start(bf16[4,1024,256]{2,1,0:T(8,128)(2,1)} %copy-done), calls=%async_computation | async-start | bytes 4194304 | tf_op jit(solution)/shard_map/all_to_all | solution.py:311
  14.6 28.3 %collective-permute-start.2 = (bf16[1024,256]{1,0:T(8,128)(2,1)S(1)}, bf16[1024,256]{1,0:T(8,128)(2,1)S(1)}, u32[]{:S(2)}, u32[]{:S(2)}) collective-permute-start(bf16[1024,256]{1,0:T(8,128)(2,1)S(1)} %get-tuple-element.16.own), channel_id=1, source_target_pairs={{8,0},{12,4},{4,8},{0,12},{9,1},{13,5},{5,9},{1,13},{10,2},{14,6},... | collective-permute-start | bytes 1572872 | tf_op jit(solution)/shard_map/ppermute | solution.py:310
  22.5 22.8 %collective-permute-start.1 = (bf16[1024,256]{1,0:T(8,128)(2,1)S(1)}, bf16[1024,256]{1,0:T(8,128)(2,1)}, u32[]{:S(2)}, u32[]{:S(2)}) collective-permute-start(bf16[1024,256]{1,0:T(8,128)(2,1)S(1)} %get-tuple-element.16.own), channel_id=1, source_target_pairs={{0,4},{4,0},{8,12},{12,8},{1,5},{5,1},{9,13},{13,9},{2,6},{6,2},{1... | collective-permute-start | bytes 1572872 | tf_op jit(solution)/shard_map/ppermute | solution.py:78
  48.2 7.4 %collective-permute-start.3 = (f32[16,136,128]{2,1,0:T(8,128)S(1)}, f32[16,136,128]{2,1,0:T(8,128)S(1)}, u32[]{:S(2)}, u32[]{:S(2)}) collective-permute-start(f32[16,136,128]{2,1,0:T(8,128)S(1)} %get-tuple-element.18), channel_id=1, source_target_pairs={{0,16},{16,0},{1,17},{17,1},{2,18},{18,2},{3,19},{19,3},{4,20},{20... | collective-permute-start | bytes 3342344 | tf_op jit(solution)/shard_map/ppermute | solution.py:78
  57.4 33.7 %all-to-all-start.1 = ((s16[16,144,128]{2,1,0:T(8,128)(2,1)}), s16[16,144,128]{2,1,0:T(8,128)(2,1)S(1)}, u32[]{:S(2)}, u32[]{:S(2)}) async-start(s16[16,144,128]{2,1,0:T(8,128)(2,1)} %encode.1), calls=%async_computation.1 | async-start | bytes 1179648 | tf_op jit(solution)/shard_map/all_to_all | solution.py:317
  91.4 9.8 %collective-permute-start.5 = (f32[128,128]{1,0:T(8,128)S(1)}, f32[128,128]{1,0:T(8,128)S(1)}, u32[]{:S(2)}, u32[]{:S(2)}) collective-permute-start(f32[128,128]{1,0:T(8,128)S(1)} %get-tuple-element.19.quad), channel_id=1, source_target_pairs={{1,48},{2,80},{3,112},{4,4},{5,36},{6,68},{7,100},{8,136},{9,168},... | collective-permute-start | bytes 196616 | tf_op jit(solution)/shard_map/ppermute | solution.py:320
  95.7 11.3 %collective-permute-start.4 = (f32[128,128]{1,0:T(8,128)S(1)}, f32[128,128]{1,0:T(8,128)S(1)}, u32[]{:S(2)}, u32[]{:S(2)}) collective-permute-start(f32[128,128]{1,0:T(8,128)S(1)} %get-tuple-element.19.quad), channel_id=1, source_target_pairs={{1,1},{2,2},{3,3},{4,128},{5,129},{6,130},{7,131},{8,260},{9,261},... | collective-permute-start | bytes 196616 | tf_op jit(solution)/shard_map/ppermute | solution.py:319

commit v5 on v4

--- a/solution.py
+++ b/solution.py
@@ -73,19 +73,25 @@
     return pairs, table
 
 
+def around(x, axis, by):
+    n = lax.axis_size(axis)
+    return lax.ppermute(x, axis, [((i + by) % n, i) for i in range(n)])
+
+
 def flipped(x, axis, bit=1):
     n = lax.axis_size(axis)
     return lax.ppermute(x, axis, [(i, i ^ bit) for i in range(n)])
 
 
-def products(where_ref, rows, own, c1, ct, keep, send):
+def products(where_ref, f0, f1, f2, f3, c1, ct, keep, send):
     x, z, core, count = where_ref[0], where_ref[1], where_ref[2], where_ref[3]
     dims = (((0,), (0,)), ((), ()))
     r = lax.broadcasted_iota(jnp.int32, (HALF, HALF), 0)
     c = lax.broadcasted_iota(jnp.int32, (HALF, HALF), 1)
     extra_row = lax.broadcasted_iota(jnp.int32, (EXTRA, HALF), 0)
     counted = jnp.where(extra_row == 1, count.astype(jnp.float32), 0.0)
-    for a in range(4):
+    for o, f in enumerate((f0, f1, f2, f3)):
+        a = lax.rem(x + o, 4)
 
         def put(zeta, q0, q1):
             slot = zeta * 4 + a
@@ -94,8 +100,8 @@
             keep[slot, HALF:] = counted
             send[slot, HALF:] = counted
 
-        lhs = rows[a]
-        for k, block in enumerate((own, c1, ct)):
+        lhs = f[...]
+        for k, block in enumerate((f0, c1, ct)):
             p = lax.dot_general(lhs, block[...], dims, preferred_element_type=jnp.float32)
             p00, p01, p10, p11 = p[:HALF, :HALF], p[:HALF, HALF:], p[HALF:, :HALF], p[HALF:, HALF:]
             if k == 0:
@@ -114,18 +120,18 @@
                 put(z ^ 3, p01, p11)
 
 
-def all_products(where, rows, own, c1, ct):
+def all_products(where, rows, c1, ct):
     shape = jax.ShapeDtypeStruct((16, HALF + EXTRA, HALF), jnp.float32)
     vmem = pl.BlockSpec(memory_space=pltpu.VMEM)
     return pl.pallas_call(
         products,
         out_shape=(shape, shape),
-        in_specs=[pl.BlockSpec(memory_space=pltpu.SMEM)] + [vmem] * 4,
+        in_specs=[pl.BlockSpec(memory_space=pltpu.SMEM)] + [vmem] * 6,
         out_specs=(vmem, vmem),
         compiler_params=pltpu.CompilerParams(vmem_limit_bytes=16 << 20),
         cost_estimate=pl.CostEstimate(flops=2 * 1024 * 1024 * 768, bytes_accessed=5 << 20, transcendentals=0),
         name="products",
-    )(where, rows, own, c1, ct)
+    )(where, *rows, c1, ct)
 
 
 def scale_of(code):
@@ -154,7 +160,7 @@
     return jnp.clip(jnp.round(v), -LEVELS, LEVELS).astype(jnp.int32).astype(jnp.int16)
 
 
-def decode(coded, quad, extra):
+def decode(coded, quad, extra, message):
     row = lax.broadcasted_iota(jnp.int32, (EXTRA, HALF), 0)
 
     def one(slot, carry):
@@ -166,7 +172,17 @@
         return total, rest
 
     start = jnp.zeros((HALF, HALF), jnp.float32), jnp.zeros((EXTRA, HALF), jnp.float32)
-    quad[...], extra[...] = lax.fori_loop(0, 16, one, start)
+    total, extra[...] = lax.fori_loop(0, 16, one, start)
+    quad[...] = total
+    most = jnp.max(jnp.abs(total), axis=0, keepdims=True)
+    code = jnp.ceil(jnp.log2(jnp.maximum(most, 1e-37)) * 256.0)
+    message[:HALF] = whole(total * (LEVELS / scale_of(code)))
+    message[HALF:] = whole(jnp.broadcast_to(code, (PACK, HALF)))
+
+
+def opened(message):
+    scale = scale_of(message[HALF:].astype(jnp.int32).astype(jnp.float32)[:1]) * (1.0 / LEVELS)
+    return message[:HALF].astype(jnp.int32).astype(jnp.float32) * scale
 
 
 def encoded(keep, got):
@@ -187,9 +203,10 @@
         out_shape=(
             jax.ShapeDtypeStruct((HALF, HALF), jnp.float32),
             jax.ShapeDtypeStruct((EXTRA, HALF), jnp.float32),
+            jax.ShapeDtypeStruct((HALF + PACK, HALF), jnp.int16),
         ),
         in_specs=[VMEM],
-        out_specs=(VMEM, VMEM),
+        out_specs=(VMEM, VMEM, VMEM),
         compiler_params=pltpu.CompilerParams(vmem_limit_bytes=8 << 20),
         cost_estimate=pl.CostEstimate(flops=2 << 20, bytes_accessed=1 << 20, transcendentals=0),
         name="decode",
@@ -200,7 +217,7 @@
     turn1, half1, turn2, diagonal = how[0] == 1, how[1], how[2] == 1, how[3] == 1
     r = lax.broadcasted_iota(jnp.int32, (HALF, HALF), 0)
     c = lax.broadcasted_iota(jnp.int32, (HALF, HALF), 1)
-    m, got1, got2 = quad[...], r1[...], r2[...]
+    m, got1, got2 = quad[...], opened(r1), opened(r2)
     turned2 = got2.T
     own = jnp.where(r <= c, m, m.T)
     cross = jnp.where(r > c, m, jnp.where(r == c, extra[0:1], turned2))
@@ -225,10 +242,9 @@
 
 
 def activated(window_of, code, weights, bias):
-    v = bias[...].astype(jnp.float32)
+    v = bias
     for lag in range(weights.shape[0]):
-        term = weights[lag : lag + 1, :].astype(jnp.float32) * window_of(lag)
-        v = v + jnp.where(code >= lag, term, 0.0)
+        v = v + jnp.where(code >= lag, weights[lag : lag + 1] * window_of(lag), 0.0)
     return jnp.where(code >= 0, v * (1.0 / (1.0 + jnp.exp(-v))), 0.0)
 
 
@@ -241,83 +257,94 @@
     return jnp.concatenate([column, column], axis=1)
 
 
-def conv_body(counts, inputs, weights, bias, doc_start, out, lead):
-    lead[...] = inputs[:16, :]
+def conv_body(counts, inputs, weights, bias, doc_start, out, lead, x_in, w_in, b_in, d_in, sems):
+    moves = [
+        pltpu.make_async_copy(src, dst, sems.at[k])
+        for k, (src, dst) in enumerate(((inputs, x_in), (weights, w_in), (bias, b_in), (doc_start, d_in)))
+    ]
+    for move in moves:
+        move.start()
+    for move in moves:
+        move.wait()
+    w = w_in[...].astype(jnp.float32)
+    b = b_in[...].reshape(1, 2 * HALF).astype(jnp.float32)
+    lead[:16] = x_in[:16, :].astype(jnp.float32)
+    lead[16:32] = codes(0, d_in, counts)[:16]
+    lead[32:36] = w
+    lead[36:37] = b
     for group in range(8):
         base = group * HALF
-        code = codes(group, doc_start, counts)
+        code = codes(group, d_in, counts)
         if group:
-            wide = inputs[base - 16 : base + HALF, :].astype(jnp.float32)
+            wide = x_in[base - 16 : base + HALF, :].astype(jnp.float32)
         else:
-            wide = jnp.concatenate([jnp.zeros((16, 2 * HALF), jnp.float32), inputs[:HALF, :].astype(jnp.float32)], axis=0)
-        value = activated(lambda lag: wide[16 - lag : 16 - lag + HALF], code, weights, bias)
+            wide = jnp.concatenate([jnp.zeros((16, 2 * HALF), jnp.float32), x_in[:HALF, :].astype(jnp.float32)], axis=0)
+        value = activated(lambda lag: wide[16 - lag : 16 - lag + HALF], code, w, b)
         out[base : base + HALF, :] = value.astype(jnp.bfloat16)
 
 
-def head_body(counts, main, lead, prior, weights, bias, doc_start, own, copies):
-    code = codes(0, doc_start, counts)[:16]
-    wide = jnp.concatenate([prior[...].astype(jnp.float32), lead[...].astype(jnp.float32)], axis=0)
-    value = activated(lambda lag: wide[8 - lag : 24 - lag], code, weights, bias)
-    head = value.astype(jnp.bfloat16)
-    rest = main[16:, :]
-    own[:16, :] = head
-    own[16:, :] = rest
-    for k in range(4):
-        copies[k, :16, :] = head
-        copies[k, 16:, :] = rest
+def head_body(main, lead, prior, own):
+    wide = jnp.concatenate([prior[...].astype(jnp.float32), lead[:16]], axis=0)
+    value = activated(lambda lag: wide[8 - lag : 24 - lag], lead[16:32], lead[32:36], lead[36:37])
+    own[:16, :] = value.astype(jnp.bfloat16)
+    own[16:, :] = main[16:, :]
 
 
 def conv_main(counts, inputs, weights, bias, doc_start):
+    fixed = [pltpu.with_memory_space_constraint(v, pltpu.HBM) for v in (inputs, weights, bias, doc_start)]
     return pl.pallas_call(
         conv_body,
         out_shape=(
             jax.ShapeDtypeStruct(inputs.shape, jnp.bfloat16),
-            jax.ShapeDtypeStruct((16, inputs.shape[1]), jnp.bfloat16),
+            jax.ShapeDtypeStruct((40, inputs.shape[1]), jnp.float32),
         ),
-        in_specs=[SMEM] + [VMEM] * 4,
+        in_specs=[SMEM] + [pl.BlockSpec(memory_space=pltpu.HBM)] * 4,
         out_specs=(VMEM, VMEM),
+        scratch_shapes=[pltpu.VMEM(v.shape, v.dtype) for v in (inputs, weights, bias, doc_start)]
+        + [pltpu.SemaphoreType.DMA((4,))],
         compiler_params=pltpu.CompilerParams(vmem_limit_bytes=8 << 20),
         cost_estimate=pl.CostEstimate(flops=8 << 20, bytes_accessed=1 << 20, transcendentals=1 << 19),
         name="conv_main",
-    )(counts, inputs, weights, bias, doc_start)
-
-
-def conv_head(counts, main, lead, prior, weights, bias, doc_start):
-    shape = jax.ShapeDtypeStruct(main.shape, jnp.bfloat16)
+    )(counts, *fixed)
+
+
+def conv_head(main, lead, prior):
     return pl.pallas_call(
         head_body,
-        out_shape=(shape, jax.ShapeDtypeStruct((4, *main.shape), jnp.bfloat16)),
-        in_specs=[SMEM] + [VMEM] * 6,
-        out_specs=(VMEM, VMEM),
+        out_shape=jax.ShapeDtypeStruct(main.shape, jnp.bfloat16),
+        in_specs=[VMEM] * 3,
+        out_specs=VMEM,
         compiler_params=pltpu.CompilerParams(vmem_limit_bytes=8 << 20),
         cost_estimate=pl.CostEstimate(flops=1 << 20, bytes_accessed=1 << 20, transcendentals=0),
         name="conv_head",
-    )(counts, main, lead, prior, weights, bias, doc_start)
+    )(main, lead, prior)
 
 
 def on_device(inputs, conv_weight, conv_bias, doc_start, counts):
     pairs, table = delivery()
-    length, width = inputs.shape
+    length, _ = inputs.shape
     core, z, x = lax.axis_index(CORE), lax.axis_index(ZL), lax.axis_index(X)
     count = counts[0]
 
     shards = lax.axis_size(SEQ)
     prior = lax.ppermute(inputs[length - 8 :], SEQ, [(i, i + 1) for i in range(shards - 1)])
-    bias, starts = conv_bias.reshape(1, width), doc_start.reshape(8, HALF)
-    main, lead = conv_main(counts, inputs, conv_weight, bias, starts)
-    own, copies = conv_head(counts, main, lead, prior, conv_weight, bias, starts)
+    starts = doc_start.reshape(8, HALF)
+    main, lead = conv_main(counts, inputs, conv_weight, conv_bias, starts)
+    own = conv_head(main, lead, prior)
 
     ct = lax.ppermute(own, ZL, [(TAU[i], i) for i in range(4)])
-    rows = lax.all_to_all(copies, X, split_axis=0, concat_axis=0, tiled=True)
+    f1 = around(own, X, 1)
+    f3 = around(own, X, 3)
+    f2 = around(own, X, 2)
     c1 = flipped(own, ZL)
 
     where = jnp.stack([x, z, core, count]).astype(jnp.int32)
-    keep, send = all_products(where, rows, own, c1, ct)
+    keep, send = all_products(where, (own, f1, f2, f3), c1, ct)
     coded = encoded(keep, flipped(send, CORE))
-    quad, extra = decoded(lax.all_to_all(coded, CHIPS, split_axis=0, concat_axis=0, tiled=True))
-
-    r1 = lax.ppermute(quad, AXES, pairs[0])
-    r2 = lax.ppermute(quad, AXES, pairs[1])
+    quad, extra, message = decoded(lax.all_to_all(coded, CHIPS, split_axis=0, concat_axis=0, tiled=True))
+
+    r1 = lax.ppermute(message, AXES, pairs[0])
+    r2 = lax.ppermute(message, AXES, pairs[1])
     how = lax.dynamic_index_in_dim(jnp.asarray(table), lax.axis_index(AXES), keepdims=False)
     return assembled(how, quad, extra, r1, r2)
 

time: 109 us -> 106 us (0.972)
  the two profiles are of different devices: /device:TPU:56 before, /device:TPU:78 now
where the time goes in v5:
time: 106 us
  waiting for transfers between devices  52 us (49%)
  starting transfers between devices  43.6 us (41%)
  Pallas kernels  8.07 us (8%)
  local copies, waits for them, and re-layouts  1.39 us (1%)
    all_to_all x1, waiting for transfers between devices, on_device(): lax.all_to_all(coded, CHIPS, split_axis=0, concat_axis=0, tiled=True)  19.9 us
    all_to_all x1, starting transfers between devices, on_device(): lax.all_to_all(coded, CHIPS, split_axis=0, concat_axis=0, tiled=True)  12.4 us
    ppermute x3, waiting for transfers between devices, around(): return lax.ppermute(x, axis, [((i + by) % n, i) for i in range(n)])  9.87 us
    ppermute x1, waiting for transfers between devices, on_device(): ct = lax.ppermute(own, ZL, [(TAU[i], i) for i in range(4)])  9.08 us
    ppermute x3, starting transfers between devices, around(): return lax.ppermute(x, axis, [((i + by) % n, i) for i in range(n)])  8.63 us
    ppermute x2, starting transfers between devices, flipped(): return lax.ppermute(x, axis, [(i, i ^ bit) for i in range(n)])  7.14 us
    ppermute x1, waiting for transfers between devices, on_device(): r1 = lax.ppermute(message, AXES, pairs[0])  6.51 us
    ppermute x2, waiting for transfers between devices, flipped(): return lax.ppermute(x, axis, [(i, i ^ bit) for i in range(n)])  6.49 us
  transfers between devices with their start and end apart: 10, of which 7 were waited for; matrix products, arithmetic and copies ran while one was open for 1% of the time, Pallas kernels for 2%

profile of v5, /device:TPU:78, one launch (start us, length us, event | category | flops | bytes accessed | tf_op | source)
XLA Modules:
  0.0 105.9 jit_solution(2888023798036968402)
XLA Ops:
  0.0 0.7 slice.3
  0.7 1.9 %collective-permute-start = (bf16[8,256]{1,0:T(8,128)(2,1)S(1)}, bf16[8,256]{1,0:T(8,128)(2,1)S(1)}, u32[]{:S(2)}, u32[]{:S(2)}) collective-permute-start(bf16[8,256]{1,0:T(8,128)(2,1)S(1)} %slice.3), channel_id=1, source_target_pairs={{0,16},{16,32},{32,48},{48,64},{64,80},{80,96},{96,112},{112,128},... | collective-permute-start | bytes 12296 | tf_op jit(solution)/shard_map/ppermute | solution.py:330
  3.3 2.1 %conv_main.1 = (bf16[1024,256]{1,0:T(8,128)(2,1)S(1)}, f32[40,256]{1,0:T(8,128)S(1)}) custom-call(s32[1]{0:T(128)S(6)} %copy.7.counts, bf16[1024,256]{1,0:T(8,128)(2,1)} %inputs.1, bf16[4,256]{1,0:T(4,128)(2,1)} %weights.1, bf16[256]{0:T(256)(128)(2,1)} %bias.1, s32[8,128]{1,0:T(8,128)} %bitcast.6), custom_call_target="tpu_custom_call" | custom-call | flops 8388608 | bytes 1048576 | tf_op jit(solution)/shard_map/conv_main/pallas_call | solution.py:295
  5.4 0.2 collective-permute-done.prior
  5.6 4.3 %collective-permute-start.5 = (bf16[1024,256]{1,0:T(8,128)(2,1)S(1)}, bf16[1024,256]{1,0:T(8,128)(2,1)S(1)}, u32[]{:S(2)}, u32[]{:S(2)}) collective-permute-start(bf16[1024,256]{1,0:T(8,128)(2,1)S(1)} %conv_head.1.f0), channel_id=1, source_target_pairs={{8,0},{12,4},{4,8},{0,12},{9,1},{13,5},{5,9},{1,13},{10,2},{14,6},... | collective-permute-start | bytes 1572872 | tf_op jit(solution)/shard_map/ppermute | solution.py:335
  9.9 5.2 %collective-permute-start.4 = (bf16[1024,256]{1,0:T(8,128)(2,1)S(1)}, bf16[1024,256]{1,0:T(8,128)(2,1)S(1)}, u32[]{:S(2)}, u32[]{:S(2)}) collective-permute-start(bf16[1024,256]{1,0:T(8,128)(2,1)S(1)} %conv_head.1.f0), channel_id=1, source_target_pairs={{0,4},{4,0},{8,12},{12,8},{1,5},{5,1},{9,13},{13,9},{2,6},{6,2},{1... | collective-permute-start | bytes 1572872 | tf_op jit(solution)/shard_map/ppermute | solution.py:83
  15.1 2.4 %collective-permute-start.3 = (bf16[1024,256]{1,0:T(8,128)(2,1)S(1)}, bf16[1024,256]{1,0:T(8,128)(2,1)S(1)}, u32[]{:S(2)}, u32[]{:S(2)}) collective-permute-start(bf16[1024,256]{1,0:T(8,128)(2,1)S(1)} %conv_head.1.f0), channel_id=1, source_target_pairs={{3,0},{0,1},{1,2},{2,3},{7,4},{4,5},{5,6},{6,7},{11,8},{8,9},{9,10... | collective-permute-start | bytes 1572872 | tf_op jit(solution)/shard_map/ppermute | solution.py:78
  17.5 4.3 %collective-permute-start.2 = (bf16[1024,256]{1,0:T(8,128)(2,1)S(1)}, bf16[1024,256]{1,0:T(8,128)(2,1)S(1)}, u32[]{:S(2)}, u32[]{:S(2)}) collective-permute-start(bf16[1024,256]{1,0:T(8,128)(2,1)S(1)} %conv_head.1.f0), channel_id=1, source_target_pairs={{2,0},{3,1},{0,2},{1,3},{6,4},{7,5},{4,6},{5,7},{10,8},{11,9},{8,1... | collective-permute-start | bytes 1572872 | tf_op jit(solution)/shard_map/ppermute | solution.py:78
  21.9 1.9 %collective-permute-start.1 = (bf16[1024,256]{1,0:T(8,128)(2,1)S(1)}, bf16[1024,256]{1,0:T(8,128)(2,1)S(1)}, u32[]{:S(2)}, u32[]{:S(2)}) collective-permute-start(bf16[1024,256]{1,0:T(8,128)(2,1)S(1)} %conv_head.1.f0), channel_id=1, source_target_pairs={{1,0},{2,1},{3,2},{0,3},{5,4},{6,5},{7,6},{4,7},{9,8},{10,9},{11,1... | collective-permute-start | bytes 1572872 | tf_op jit(solution)/shard_map/ppermute | solution.py:78
  23.9 9.1 %collective-permute-done.5.ct = bf16[1024,256]{1,0:T(8,128)(2,1)S(1)} collective-permute-done((bf16[1024,256]{1,0:T(8,128)(2,1)S(1)}, bf16[1024,256]{1,0:T(8,128)(2,1)S(1)}, u32[]{:S(2)}, u32[]{:S(2)}) %collective-permute-start.5) | collective-permute-done | bytes 524320 | tf_op jit(solution)/shard_map/ppermute | solution.py:335
  32.9 3.8 %collective-permute-done.4.c1 = bf16[1024,256]{1,0:T(8,128)(2,1)S(1)} collective-permute-done((bf16[1024,256]{1,0:T(8,128)(2,1)S(1)}, bf16[1024,256]{1,0:T(8,128)(2,1)S(1)}, u32[]{:S(2)}, u32[]{:S(2)}) %collective-permute-start.4) | collective-permute-done | bytes 524320 | tf_op jit(solution)/shard_map/ppermute | solution.py:83
  36.8 9.9 %collective-permute-done.1.f1 = bf16[1024,256]{1,0:T(8,128)(2,1)S(1)} collective-permute-done((bf16[1024,256]{1,0:T(8,128)(2,1)S(1)}, bf16[1024,256]{1,0:T(8,128)(2,1)S(1)}, u32[]{:S(2)}, u32[]{:S(2)}) %collective-permute-start.1) | collective-permute-done | bytes 524320 | tf_op jit(solution)/shard_map/ppermute | solution.py:78
  46.6 2.4 %products.1 = (f32[16,136,128]{2,1,0:T(8,128)S(1)}, f32[16,136,128]{2,1,0:T(8,128)S(1)}) custom-call(s32[4]{0:T(128)S(1)} %pad_add_fusion.where_ref, bf16[1024,256]{1,0:T(8,128)(2,1)S(1)} %conv_head.1.f0, bf16[1024,256]{1,0:T(8,128)(2,1)S(1)} %collective-permute-done.1.f1, bf16[1024,256]{1,0:T(8,128)(2,1)S(1)} %collective-permute-done.2.f2, ...), custom_call_target="tpu_custom_call" | custom-call | flops 1610612736 | bytes 5242880 | tf_op jit(solution)/shard_map/products/pallas_call | solution.py:126
  49.1 2.0 %collective-permute-start.6 = (f32[16,136,128]{2,1,0:T(8,128)S(1)}, f32[16,136,128]{2,1,0:T(8,128)S(1)}, u32[]{:S(2)}, u32[]{:S(2)}) collective-permute-start(f32[16,136,128]{2,1,0:T(8,128)S(1)} %get-tuple-element.15), channel_id=1, source_target_pairs={{0,16},{16,0},{1,17},{17,1},{2,18},{18,2},{3,19},{19,3},{4,20},{20... | collective-permute-start | bytes 3342344 | tf_op jit(solution)/shard_map/ppermute | solution.py:83
  51.0 2.7 %collective-permute-done.6.got = f32[16,136,128]{2,1,0:T(8,128)S(1)} collective-permute-done((f32[16,136,128]{2,1,0:T(8,128)S(1)}, f32[16,136,128]{2,1,0:T(8,128)S(1)}, u32[]{:S(2)}, u32[]{:S(2)}) %collective-permute-start.6) | collective-permute-done | bytes 1114144 | tf_op jit(solution)/shard_map/ppermute | solution.py:83
  53.7 1.7 %encode.1 = s16[16,144,128]{2,1,0:T(8,128)(2,1)} custom-call(f32[16,136,128]{2,1,0:T(8,128)S(1)} %get-tuple-element.14.keep, f32[16,136,128]{2,1,0:T(8,128)S(1)} %collective-permute-done.6.got), custom_call_target="tpu_custom_call" | custom-call | flops 2097152 | bytes 3145728 | tf_op jit(solution)/shard_map/encode/pallas_call | solution.py:189
  55.4 12.4 %all-to-all-start = ((s16[16,144,128]{2,1,0:T(8,128)(2,1)}), s16[16,144,128]{2,1,0:T(8,128)(2,1)S(1)}, u32[]{:S(2)}, u32[]{:S(2)}) async-start(s16[16,144,128]{2,1,0:T(8,128)(2,1)} %encode.1), calls=%async_computation | async-start | bytes 1179648 | tf_op jit(solution)/shard_map/all_to_all | solution.py:344
  67.8 19.9 %all-to-all-done.coded = s16[16,144,128]{2,1,0:T(8,128)(2,1)S(1)} async-done(((s16[16,144,128]{2,1,0:T(8,128)(2,1)}), s16[16,144,128]{2,1,0:T(8,128)(2,1)S(1)}, u32[]{:S(2)}, u32[]{:S(2)}) %all-to-all-start) | async-done | bytes 589856 | tf_op jit(solution)/shard_map/all_to_all | solution.py:344
  87.7 0.4 decode.1
  88.1 5.7 %collective-permute-start.8 = (s16[144,128]{1,0:T(8,128)(2,1)S(1)}, s16[144,128]{1,0:T(8,128)(2,1)S(1)}, u32[]{:S(2)}, u32[]{:S(2)}) collective-permute-start(s16[144,128]{1,0:T(8,128)(2,1)S(1)} %get-tuple-element.18), channel_id=1, source_target_pairs={{1,48},{2,80},{3,112},{4,4},{5,36},{6,68},{7,100},{8,136},{9,168},... | collective-permute-start | bytes 110600 | tf_op jit(solution)/shard_map/ppermute | solution.py:347
  93.9 3.4 %collective-permute-start.7 = (s16[144,128]{1,0:T(8,128)(2,1)S(1)}, s16[144,128]{1,0:T(8,128)(2,1)S(1)}, u32[]{:S(2)}, u32[]{:S(2)}) collective-permute-start(s16[144,128]{1,0:T(8,128)(2,1)S(1)} %get-tuple-element.18), channel_id=1, source_target_pairs={{1,1},{2,2},{3,3},{4,128},{5,129},{6,130},{7,131},{8,260},{9,261},... | collective-permute-start | bytes 110600 | tf_op jit(solution)/shard_map/ppermute | solution.py:346
  97.3 0.7 dynamic-slice_bitcast_fusion.how
  98.0 6.5 %collective-permute-done.7.r1 = s16[144,128]{1,0:T(8,128)(2,1)S(1)} collective-permute-done((s16[144,128]{1,0:T(8,128)(2,1)S(1)}, s16[144,128]{1,0:T(8,128)(2,1)S(1)}, u32[]{:S(2)}, u32[]{:S(2)}) %collective-permute-start.7) | collective-permute-done | bytes 36896 | tf_op jit(solution)/shard_map/ppermute | solution.py:346
  104.6 1.3 %assemble.1 = f32[128,256]{1,0:T(8,128)} custom-call(s32[4]{0:T(128)S(1)} %dynamic-slice_bitcast_fusion.how, f32[128,128]{1,0:T(8,128)S(1)} %get-tuple-element.16.quad, f32[8,128]{1,0:T(8,128)S(1)} %get-tuple-element.17.extra, s16[144,128]{1,0:T(8,128)(2,1)S(1)} %collective-permute-done.7.r1, s16[144,128]{1,0:T(8,128)(2,1)S(1)} %collective-permute-done.8.r2), custom_call_target="tpu_custom_call" | custom-call | flops 1048576 | bytes 524288 | tf_op jit(solution)/shard_map/assemble/pallas_call | solution.py:233
  (5 shorter events, 0.1 us)
Async XLA Ops:
  0.7 4.9 %collective-permute-start = (bf16[8,256]{1,0:T(8,128)(2,1)S(1)}, bf16[8,256]{1,0:T(8,128)(2,1)S(1)}, u32[]{:S(2)}, u32[]{:S(2)}) collective-permute-start(bf16[8,256]{1,0:T(8,128)(2,1)S(1)} %slice.3), channel_id=1, source_target_pairs={{0,16},{16,32},{32,48},{48,64},{64,80},{80,96},{96,112},{112,128},... | collective-permute-start | bytes 12296 | tf_op jit(solution)/shard_map/ppermute | solution.py:330
  5.6 27.3 %collective-permute-start.5 = (bf16[1024,256]{1,0:T(8,128)(2,1)S(1)}, bf16[1024,256]{1,0:T(8,128)(2,1)S(1)}, u32[]{:S(2)}, u32[]{:S(2)}) collective-permute-start(bf16[1024,256]{1,0:T(8,128)(2,1)S(1)} %conv_head.1.f0), channel_id=1, source_target_pairs={{8,0},{12,4},{4,8},{0,12},{9,1},{13,5},{5,9},{1,13},{10,2},{14,6},... | collective-permute-start | bytes 1572872 | tf_op jit(solution)/shard_map/ppermute | solution.py:335
  9.9 26.8 %collective-permute-start.4 = (bf16[1024,256]{1,0:T(8,128)(2,1)S(1)}, bf16[1024,256]{1,0:T(8,128)(2,1)S(1)}, u32[]{:S(2)}, u32[]{:S(2)}) collective-permute-start(bf16[1024,256]{1,0:T(8,128)(2,1)S(1)} %conv_head.1.f0), channel_id=1, source_target_pairs={{0,4},{4,0},{8,12},{12,8},{1,5},{5,1},{9,13},{13,9},{2,6},{6,2},{1... | collective-permute-start | bytes 1572872 | tf_op jit(solution)/shard_map/ppermute | solution.py:83
  15.1 21.6 %collective-permute-start.3 = (bf16[1024,256]{1,0:T(8,128)(2,1)S(1)}, bf16[1024,256]{1,0:T(8,128)(2,1)S(1)}, u32[]{:S(2)}, u32[]{:S(2)}) collective-permute-start(bf16[1024,256]{1,0:T(8,128)(2,1)S(1)} %conv_head.1.f0), channel_id=1, source_target_pairs={{3,0},{0,1},{1,2},{2,3},{7,4},{4,5},{5,6},{6,7},{11,8},{8,9},{9,10... | collective-permute-start | bytes 1572872 | tf_op jit(solution)/shard_map/ppermute | solution.py:78
  17.5 19.2 %collective-permute-start.2 = (bf16[1024,256]{1,0:T(8,128)(2,1)S(1)}, bf16[1024,256]{1,0:T(8,128)(2,1)S(1)}, u32[]{:S(2)}, u32[]{:S(2)}) collective-permute-start(bf16[1024,256]{1,0:T(8,128)(2,1)S(1)} %conv_head.1.f0), channel_id=1, source_target_pairs={{2,0},{3,1},{0,2},{1,3},{6,4},{7,5},{4,6},{5,7},{10,8},{11,9},{8,1... | collective-permute-start | bytes 1572872 | tf_op jit(solution)/shard_map/ppermute | solution.py:78
  21.9 24.8 %collective-permute-start.1 = (bf16[1024,256]{1,0:T(8,128)(2,1)S(1)}, bf16[1024,256]{1,0:T(8,128)(2,1)S(1)}, u32[]{:S(2)}, u32[]{:S(2)}) collective-permute-start(bf16[1024,256]{1,0:T(8,128)(2,1)S(1)} %conv_head.1.f0), channel_id=1, source_target_pairs={{1,0},{2,1},{3,2},{0,3},{5,4},{6,5},{7,6},{4,7},{9,8},{10,9},{11,1... | collective-permute-start | bytes 1572872 | tf_op jit(solution)/shard_map/ppermute | solution.py:78
  49.1 4.6 %collective-permute-start.6 = (f32[16,136,128]{2,1,0:T(8,128)S(1)}, f32[16,136,128]{2,1,0:T(8,128)S(1)}, u32[]{:S(2)}, u32[]{:S(2)}) collective-permute-start(f32[16,136,128]{2,1,0:T(8,128)S(1)} %get-tuple-element.15), channel_id=1, source_target_pairs={{0,16},{16,0},{1,17},{17,1},{2,18},{18,2},{3,19},{19,3},{4,20},{20... | collective-permute-start | bytes 3342344 | tf_op jit(solution)/shard_map/ppermute | solution.py:83
  55.4 32.3 %all-to-all-start = ((s16[16,144,128]{2,1,0:T(8,128)(2,1)}), s16[16,144,128]{2,1,0:T(8,128)(2,1)S(1)}, u32[]{:S(2)}, u32[]{:S(2)}) async-start(s16[16,144,128]{2,1,0:T(8,128)(2,1)} %encode.1), calls=%async_computation | async-start | bytes 1179648 | tf_op jit(solution)/shard_map/all_to_all | solution.py:344
  88.1 9.9 %collective-permute-start.8 = (s16[144,128]{1,0:T(8,128)(2,1)S(1)}, s16[144,128]{1,0:T(8,128)(2,1)S(1)}, u32[]{:S(2)}, u32[]{:S(2)}) collective-permute-start(s16[144,128]{1,0:T(8,128)(2,1)S(1)} %get-tuple-element.18), channel_id=1, source_target_pairs={{1,48},{2,80},{3,112},{4,4},{5,36},{6,68},{7,100},{8,136},{9,168},... | collective-permute-start | bytes 110600 | tf_op jit(solution)/shard_map/ppermute | solution.py:347
  93.9 10.7 %collective-permute-start.7 = (s16[144,128]{1,0:T(8,128)(2,1)S(1)}, s16[144,128]{1,0:T(8,128)(2,1)S(1)}, u32[]{:S(2)}, u32[]{:S(2)}) collective-permute-start(s16[144,128]{1,0:T(8,128)(2,1)S(1)} %get-tuple-element.18), channel_id=1, source_target_pairs={{1,1},{2,2},{3,3},{4,128},{5,129},{6,130},{7,131},{8,260},{9,261},... | collective-permute-start | bytes 110600 | tf_op jit(solution)/shard_map/ppermute | solution.py:346
